TPU v7x, 32 devices: a whole 2x2x4 slice. The times are simulated.
32 devices in a mesh: groups: 2 (over y), seq: 16 (over z, x, core).
Axes of the slice: x: 2, y: 2, z: 4, core: 2. Of those that a mesh axis runs over, the one named last changes fastest.
Arguments:
- queries: bfloat16 [8192, 4096], P(('groups', 'seq')), parts along dimension 0
- new_keys: bfloat16 [8192, 1024], P(('groups', 'seq')), parts along dimension 0
- new_values: bfloat16 [8192, 1024], P(('groups', 'seq')), parts along dimension 0, may hold values from -6 to 6
- pool_keys: bfloat16 [672, 16, 1024], P(('groups', 'seq')), parts along dimension 0, may hold values from -10 to 10
- pool_values: bfloat16 [672, 16, 1024], P(('groups', 'seq')), parts along dimension 0, may hold values from -6 to 6
- prefix_len: int32 [32], P(('groups', 'seq')), parts along dimension 0, may hold values from 1 to 80
- new_len: int32 [32], P(('groups', 'seq')), parts along dimension 0, may hold values from 128 to 256
- page_holder: int32 [32, 5], P(('groups', 'seq')), parts along dimension 0, may hold values from 0 to 15, as said below
- page_slot: int32 [32, 5], P(('groups', 'seq')), parts along dimension 0, may hold values from 0 to 20, as said below
- new_holder: int32 [32, 16], P(('groups', 'seq')), parts along dimension 0, may hold values from 0 to 15, as said below
- new_slot: int32 [32, 16], P(('groups', 'seq')), parts along dimension 0, may hold values from 0 to 20
Outputs:
- attention_out: bfloat16 [8192, 4096], P(('groups', 'seq')), parts along dimension 0
- pool_keys_out: bfloat16 [672, 16, 1024], P(('groups', 'seq')), parts along dimension 0
- pool_values_out: bfloat16 [672, 16, 1024], P(('groups', 'seq')), parts along dimension 0
There are 2 independent parts, one for each index of `groups`. A program takes and returns all parts, laid end to end along the dimension named above; each array names one. Nothing has to cross between parts.
Inputs may be any that keep to these rules, and one draw needn't show every extreme that they name: `page_holder`: the 5 pages named for one conversation lie on distinct devices. No pool slot is named twice by page_slot and new_slot together, and no slot named by new_slot is named by page_slot. `new_holder`: the 16 pages of one conversation's new turn go to distinct devices.
All inputs are finite; a program needn't handle non-finite values.
Results may differ from a plain program's by a relative error of at most 0.0027.
Values may be sent and summed in bfloat16 or wider, within the bound.
No kernel may reach another device: no remote copies, remote signals or barrier semaphores. Data moves between devices by JAX's collectives and lax.ppermute only.
A program may use at most 128 MiB of HBM per device.

v0:
```python
import math

import jax
import jax.numpy as jnp
from jax import lax
from jax.sharding import PartitionSpec as P

HEADS = 32
KV_HEADS = 8
HEAD = 128


def score_block(query_block, key_slice, scaling):
    return (
        jnp.einsum("tgd,kd->tgk", query_block, key_slice, preferred_element_type=jnp.float32)
        * scaling
    )


def fresh_scores_all(queries, new_keys, fresh_live, scaling):
    group_size = HEADS // KV_HEADS
    span_rows = queries.shape[0]
    fresh_parts = []
    for head_group in range(KV_HEADS):
        first_col = head_group * group_size * HEAD
        query_block = queries[:, first_col : first_col + group_size * HEAD].reshape(
            span_rows, group_size, HEAD
        )
        key_slice = new_keys[:, head_group * HEAD : (head_group + 1) * HEAD]
        scores = score_block(query_block, key_slice, scaling)
        fresh_parts.append(jnp.where(fresh_live[:, None, :], scores, -jnp.inf))
    return fresh_parts


def shards(
    queries,
    new_keys,
    new_values,
    pool_keys,
    pool_values,
    prefix_len,
    new_len,
    page_holder,
    page_slot,
    new_holder,
    new_slot,
):
    devices = lax.axis_size("seq")
    pool_count = pool_keys.shape[0]
    page_rows = pool_keys.shape[1]
    kv_width = pool_keys.shape[2]
    span_rows = queries.shape[0]
    fresh_pages = span_rows // page_rows
    prefix_pages = page_holder.shape[1]
    group_size = HEADS // KV_HEADS
    scaling = 1.0 / math.sqrt(HEAD)
    peer_ids = jnp.arange(devices, dtype=jnp.int32)
    prefix_tokens = prefix_len[0]
    fresh_tokens = new_len[0]
    holders = page_holder[0]
    page_live = jnp.arange(prefix_pages, dtype=jnp.int32) * page_rows < prefix_tokens
    wanted = (holders[None, :] == peer_ids[:, None]) & page_live[None, :]
    request = jnp.sum(jnp.where(wanted, page_slot[0][None, :] + 1, 0), axis=1)
    token_pos = jnp.arange(span_rows, dtype=jnp.int32)
    row_keep = (token_pos < fresh_tokens)[:, None]
    fresh_live = (token_pos[None, :] <= token_pos[:, None]) & (token_pos[None, :] < fresh_tokens)
    kept_keys = jnp.where(row_keep, new_keys, 0).reshape(fresh_pages, page_rows * kv_width)
    kept_values = jnp.where(row_keep, new_values, 0).reshape(fresh_pages, page_rows * kv_width)
    target_hot = new_holder[0][None, :] == peer_ids[:, None]
    hot_matrix = target_hot.astype(jnp.bfloat16)
    out_keys = jnp.dot(hot_matrix, kept_keys, preferred_element_type=jnp.float32).astype(
        jnp.bfloat16
    )
    out_values = jnp.dot(hot_matrix, kept_values, preferred_element_type=jnp.float32).astype(
        jnp.bfloat16
    )
    out_slots = jnp.sum(jnp.where(target_hot, new_slot[0][None, :] + 1, 0), axis=1)
    slot_column = out_slots.astype(jnp.bfloat16)[:, None]
    incoming = (
        lax.all_to_all(
            request.astype(jnp.bfloat16)[:, None], "seq", split_axis=0, concat_axis=0, tiled=True
        ),
        lax.all_to_all(out_keys, "seq", split_axis=0, concat_axis=0, tiled=True),
        lax.all_to_all(out_values, "seq", split_axis=0, concat_axis=0, tiled=True),
        lax.all_to_all(slot_column, "seq", split_axis=0, concat_axis=0, tiled=True),
    )
    asked_slots = incoming[0][:, 0].astype(jnp.int32)
    returned = (incoming[1], incoming[2], incoming[3][:, 0].astype(jnp.int32))
    chosen = jnp.maximum(asked_slots - 1, 0)
    sending = (asked_slots > 0)[:, None, None]
    send_keys = jnp.where(sending, jnp.take(pool_keys, chosen, axis=0), 0)
    send_values = jnp.where(sending, jnp.take(pool_values, chosen, axis=0), 0)
    received_keys, received_values = (
        lax.all_to_all(send_keys, "seq", split_axis=0, concat_axis=0, tiled=True),
        lax.all_to_all(send_values, "seq", split_axis=0, concat_axis=0, tiled=True),
    )
    prefix_keys = jnp.take(received_keys, holders, axis=0).reshape(
        prefix_pages * page_rows, kv_width
    )
    prefix_values = jnp.take(received_values, holders, axis=0).reshape(
        prefix_pages * page_rows, kv_width
    )
    prefix_live = jnp.arange(prefix_pages * page_rows, dtype=jnp.int32) < prefix_tokens
    fresh_parts = fresh_scores_all(queries, new_keys, fresh_live, scaling)
    blocks = []
    for head_group in range(KV_HEADS):
        first_col = head_group * group_size * HEAD
        query_block = queries[:, first_col : first_col + group_size * HEAD].reshape(
            span_rows, group_size, HEAD
        )
        key_first = head_group * HEAD
        prefix_scores = score_block(
            query_block, prefix_keys[:, key_first : key_first + HEAD], scaling
        )
        prefix_scores = jnp.where(prefix_live[None, None, :], prefix_scores, -jnp.inf)
        fresh_part = fresh_parts[head_group]
        row_top = jnp.maximum(jnp.max(prefix_scores, axis=-1), jnp.max(fresh_part, axis=-1))[
            ..., None
        ]
        prefix_weights = jnp.exp(prefix_scores - row_top)
        fresh_weights = jnp.exp(fresh_part - row_top)
        weight_sum = jnp.sum(prefix_weights, axis=-1) + jnp.sum(fresh_weights, axis=-1)
        weighted = jnp.einsum(
            "tgk,kd->tgd",
            prefix_weights.astype(jnp.bfloat16),
            prefix_values[:, key_first : key_first + HEAD],
            preferred_element_type=jnp.float32,
        )
        weighted = weighted + jnp.einsum(
            "tgk,kd->tgd",
            fresh_weights.astype(jnp.bfloat16),
            new_values[:, key_first : key_first + HEAD],
            preferred_element_type=jnp.float32,
        )
        blocks.append((weighted / weight_sum[..., None]).reshape(span_rows, group_size * HEAD))
    attention_out = jnp.where(row_keep, jnp.concatenate(blocks, axis=1), 0.0).astype(jnp.bfloat16)
    slot_target = jnp.where(returned[2] > 0, returned[2] - 1, pool_count)
    pool_keys_out = pool_keys.at[slot_target].set(
        returned[0].reshape(devices, page_rows, kv_width), mode="drop"
    )
    pool_values_out = pool_values.at[slot_target].set(
        returned[1].reshape(devices, page_rows, kv_width), mode="drop"
    )
    return (attention_out, pool_keys_out, pool_values_out)


def solution(mesh):
    in_specs = (
        P(("groups", "seq"), None),
        P(("groups", "seq"), None),
        P(("groups", "seq"), None),
        P(("groups", "seq"), None, None),
        P(("groups", "seq"), None, None),
        P(("groups", "seq")),
        P(("groups", "seq")),
        P(("groups", "seq"), None),
        P(("groups", "seq"), None),
        P(("groups", "seq"), None),
        P(("groups", "seq"), None),
    )
    out_specs = (
        P(("groups", "seq"), None),
        P(("groups", "seq"), None, None),
        P(("groups", "seq"), None, None),
    )
    return jax.shard_map(shards, mesh=mesh, in_specs=in_specs, out_specs=out_specs, check_vma=False)
```

profile of v0, /device:TPU:0, one launch (start us, length us, event | category | flops | bytes accessed | tf_op | source)
XLA Modules:
  0.0 176.7 jit_solution(17692647910768368222)
XLA Ops:
  0.7 2.0 %copy.299 = bf16[21,16,1024]{2,1,0:T(8,128)(2,1)} copy(bf16[21,16,1024]{2,1,0:T(8,128)(2,1)} %param.18) | data formatting | bytes 1376256
  5.3 7.4 %all-to-all-start = ((bf16[16,1,1]{2,1,0:T(2,128)(2,1)}), bf16[16,1,1]{2,1,0:T(2,128)(2,1)S(1)}, u32[]{:S(2)}, u32[]{:S(2)}) async-start(bf16[16,1,1]{2,1,0:T(2,128)(2,1)} %copy.190), calls=%async_computation | async-start | bytes 16384 | tf_op jit(solution)/shard_map/all_to_all | solution.py:80
  12.7 2.5 %fusion.144 = (bf16[256,512]{1,0:T(8,128)(2,1)S(1)}, bf16[256,512]{1,0:T(8,128)(2,1)}, bf16[256,512]{1,0:T(8,128)(2,1)S(1)}, bf16[256,512]{1,0:T(8,128)(2,1)S(1)...) fusion(bf16[256,4096]{1,0:T(8,128)(2,1)} %param.15), kind=kLoop, calls=%fused_computation.229 | loop fusion | bytes 4194304 | tf_op jit(solution)/shard_map/slice | solution.py:108
  20.3 1.3 reshape.299
  23.2 2.0 %reduce.8 = bf16[16,16384]{1,0:T(8,128)(2,1)S(1)} reduce(bf16[16,1,16384]{2,0,1:T(8,128)(2,1)} %fusion, bf16[]{:T(256)} %broadcast.241), dimensions={1}, to_apply=%copy.240.reduce_sub_computation | reduce | bytes 1048578 | tf_op jit(solution)/shard_map/all_to_all | solution.py:83
  25.2 1.2 reshape.400
  28.7 6.0 %all-to-all-start.3 = ((bf16[16,1,1]{2,1,0:T(2,128)(2,1)}), bf16[16,1,1]{2,1,0:T(2,128)(2,1)S(1)}, u32[]{:S(2)}, u32[]{:S(2)}) async-start(bf16[16,1,1]{2,1,0:T(2,128)(2,1)} %copy.239), calls=%async_computation.3 | async-start | bytes 16384 | tf_op jit(solution)/shard_map/all_to_all | solution.py:85
  34.7 1.2 reshape.402
  35.9 5.3 %all-to-all-done.3 = bf16[16,1,1]{2,1,0:T(2,128)(2,1)S(1)} async-done(((bf16[16,1,1]{2,1,0:T(2,128)(2,1)}), bf16[16,1,1]{2,1,0:T(2,128)(2,1)S(1)}, u32[]{:S(2)}, u32[]{:S(2)}) %all-to-all-start.3) | async-done | bytes 64 | tf_op jit(solution)/shard_map/all_to_all | solution.py:85
  41.2 4.2 %all-to-all-start.4 = ((bf16[16,2,8192]{2,1,0:T(2,128)(2,1)}), bf16[16,2,8192]{2,1,0:T(2,128)(2,1)}, u32[]{:S(2)}, u32[]{:S(2)}) async-start(bf16[16,2,8192]{2,1,0:T(2,128)(2,1)} %reshape.400), calls=%async_computation.4 | async-start | bytes 1048576 | tf_op jit(solution)/shard_map/all_to_all | solution.py:83
  45.4 1.3 fusion.160
  47.0 1.3 fusion.156
  48.3 11.4 %all-to-all-done.4 = bf16[16,2,8192]{2,1,0:T(2,128)(2,1)} async-done(((bf16[16,2,8192]{2,1,0:T(2,128)(2,1)}), bf16[16,2,8192]{2,1,0:T(2,128)(2,1)}, u32[]{:S(2)}, u32[]{:S(2)}) %all-to-all-start.4) | async-done | bytes 524320 | tf_op jit(solution)/shard_map/all_to_all | solution.py:83
  59.7 4.2 %all-to-all-start.5 = ((bf16[16,2,8192]{2,1,0:T(2,128)(2,1)}), bf16[16,2,8192]{2,1,0:T(2,128)(2,1)}, u32[]{:S(2)}, u32[]{:S(2)}) async-start(bf16[16,2,8192]{2,1,0:T(2,128)(2,1)} %reshape.402), calls=%async_computation.5 | async-start | bytes 1048576 | tf_op jit(solution)/shard_map/all_to_all | solution.py:84
  64.3 2.5 %gather_fusion = bf16[16,16,1024]{2,1,0:T(8,128)(2,1)} fusion(bf16[21,16,1024]{2,1,0:T(8,128)(2,1)} %copy.299, s32[1024]{0:T(1024)S(1)} %pad_clamp_fusion.1), kind=kCustom, calls=%fused_computation.clone | custom fusion | bytes 1048640 | tf_op jit(solution)/shard_map/jit(_take)/gather | solution.py:91
  66.8 1.4 gather_fusion.2
  68.6 2.4 %select_select_fusion = (bf16[16,16,1024]{2,1,0:T(8,128)(2,1)}, bf16[16,16,1024]{2,1,0:T(8,128)(2,1)}) fusion(bf16[16,16,1024]{2,1,0:T(8,128)(2,1)} %gather_fusion.2, pred[16]{0:T(512)(128)(4,1)S(1)} %compare_and_fusion.1, pred[16]{0:T(512)(128)(4,1)S(1)} %compare_reduce_fusion, bf16[16,16,1024]{2,1,0:T(8,128)(2,1)} %gather_fusion), kind=kLoop, calls=%fused_computation.99 | loop fusion | flops 1048576 | bytes 2097184 | tf_op jit(solution)/shard_map/jit(_where)/select_n | solution.py:92
  71.0 7.2 %all-to-all-done.5 = bf16[16,2,8192]{2,1,0:T(2,128)(2,1)} async-done(((bf16[16,2,8192]{2,1,0:T(2,128)(2,1)}), bf16[16,2,8192]{2,1,0:T(2,128)(2,1)}, u32[]{:S(2)}, u32[]{:S(2)}) %all-to-all-start.5) | async-done | bytes 524320 | tf_op jit(solution)/shard_map/all_to_all | solution.py:84
  78.2 4.2 %all-to-all-start.1 = ((bf16[16,16,1024]{2,1,0:T(8,128)(2,1)}), bf16[16,16,1024]{2,1,0:T(8,128)(2,1)}, u32[]{:S(2)}, u32[]{:S(2)}) async-start(bf16[16,16,1024]{2,1,0:T(8,128)(2,1)} %get-tuple-element.14), calls=%async_computation.1 | async-start | bytes 1048576 | tf_op jit(solution)/shard_map/all_to_all | solution.py:94
  82.5 2.2 %fusion.154 = (f32[256,4]{0,1:T(4,128)S(1)}, f32[256,4,256]{0,2,1:T(8,128)}) fusion(bf16[256,4,128]{0,2,1:T(8,128)(2,1)S(1)} %bitcast.222, bf16[256,1024]{1,0:T(8,128)(2,1)} %param.16, pred[256,256]{0,1:T(8,128)(4,1)S(1)} %fusion.90), kind=kOutput, calls=%fused_computation.239 | convolution fusion | flops 67894272 | bytes 1445888 | tf_op jit(solution)/shard_map/tgd,kd->tgk/dot_general | solution.py:15
  84.6 2.1 %fusion.152 = (f32[256,4]{0,1:T(4,128)S(1)}, f32[256,4,256]{0,2,1:T(8,128)}) fusion(bf16[256,4,128]{0,2,1:T(8,128)(2,1)S(1)} %bitcast.220, bf16[256,1024]{1,0:T(8,128)(2,1)} %param.16, pred[256,256]{0,1:T(8,128)(4,1)S(1)} %fusion.90), kind=kOutput, calls=%fused_computation.237 | convolution fusion | flops 67894272 | bytes 1445888 | tf_op jit(solution)/shard_map/tgd,kd->tgk/dot_general | solution.py:15
  87.9 8.8 %all-to-all-done.1 = bf16[16,16,1024]{2,1,0:T(8,128)(2,1)} async-done(((bf16[16,16,1024]{2,1,0:T(8,128)(2,1)}), bf16[16,16,1024]{2,1,0:T(8,128)(2,1)}, u32[]{:S(2)}, u32[]{:S(2)}) %all-to-all-start.1) | async-done | bytes 524320 | tf_op jit(solution)/shard_map/all_to_all | solution.py:94
  96.7 4.4 %all-to-all-start.2 = ((bf16[16,16,1024]{2,1,0:T(8,128)(2,1)}), bf16[16,16,1024]{2,1,0:T(8,128)(2,1)}, u32[]{:S(2)}, u32[]{:S(2)}) async-start(bf16[16,16,1024]{2,1,0:T(8,128)(2,1)} %get-tuple-element.13), calls=%async_computation.2 | async-start | bytes 1048576 | tf_op jit(solution)/shard_map/all_to_all | solution.py:95
  101.2 1.8 %copy.268 = bf16[256,512]{0,1:T(8,128)(2,1)} copy(bf16[256,512]{1,0:T(8,128)(2,1)} %get-tuple-element.11) | data formatting | bytes 524288
  103.0 1.8 %copy.266 = bf16[256,512]{0,1:T(8,128)(2,1)} copy(bf16[256,512]{1,0:T(8,128)(2,1)} %get-tuple-element.12) | data formatting | bytes 524288
  104.8 2.3 %fusion.148 = (f32[256,4]{0,1:T(4,128)S(1)}, f32[256,4,256]{0,2,1:T(8,128)}) fusion(bf16[256,4,128]{0,2,1:T(8,128)(2,1)} %bitcast.232, bf16[256,1024]{1,0:T(8,128)(2,1)} %param.16, pred[256,256]{0,1:T(8,128)(4,1)S(1)} %fusion.90), kind=kOutput, calls=%fused_computation.233 | convolution fusion | flops 67894272 | bytes 1445888 | tf_op jit(solution)/shard_map/tgd,kd->tgk/dot_general | solution.py:15
  107.0 2.3 %fusion.146 = (f32[256,4]{0,1:T(4,128)S(1)}, f32[256,4,256]{0,2,1:T(8,128)}) fusion(bf16[256,4,128]{0,2,1:T(8,128)(2,1)} %bitcast.230, bf16[256,1024]{1,0:T(8,128)(2,1)} %param.16, pred[256,256]{0,1:T(8,128)(4,1)S(1)} %fusion.90), kind=kOutput, calls=%fused_computation.231 | convolution fusion | flops 67894272 | bytes 1445888 | tf_op jit(solution)/shard_map/tgd,kd->tgk/dot_general | solution.py:15
  109.7 3.5 %reshape.401 = bf16[16,1,16384]{2,1,0:T(2,128)(2,1)} reshape(bf16[16,2,8192]{2,1,0:T(2,128)(2,1)} %all-to-all-done.4) | data formatting | bytes 1048576
  113.2 5.1 %reduce.3 = bf16[16,16384]{1,0:T(8,128)(2,1)} reduce(bf16[16,1,16384]{2,1,0:T(2,128)(2,1)} %reshape.401, bf16[]{:T(256)} %constant.55), dimensions={1}, to_apply=%all_to_all.31.reduce_sub_computation | reduce | bytes 1048578 | tf_op jit(solution)/shard_map/all_to_all | solution.py:83
  118.2 2.2 %copy.282 = bf16[2,8,16,1024]{3,2,1,0:T(8,128)(2,1)} copy(bf16[2,8,16,1024]{3,1,2,0:T(8,128)(2,1)} %bitcast.237) | data formatting | bytes 1048576
  120.4 3.5 %reshape.403 = bf16[16,1,16384]{2,1,0:T(2,128)(2,1)} reshape(bf16[16,2,8192]{2,1,0:T(2,128)(2,1)} %all-to-all-done.5) | data formatting | bytes 1048576
  123.9 5.1 %reduce.4 = bf16[16,16384]{1,0:T(8,128)(2,1)} reduce(bf16[16,1,16384]{2,1,0:T(2,128)(2,1)} %reshape.403, bf16[]{:T(256)} %constant.55), dimensions={1}, to_apply=%all_to_all.33.reduce_sub_computation | reduce | bytes 1048578 | tf_op jit(solution)/shard_map/all_to_all | solution.py:84
  129.0 2.1 %copy.283 = bf16[2,8,16,1024]{3,2,1,0:T(8,128)(2,1)} copy(bf16[2,8,16,1024]{3,1,2,0:T(8,128)(2,1)} %bitcast.236) | data formatting | bytes 1048576
  131.1 2.9 %scatter_fusion = bf16[21,16,1024]{2,1,0:T(8,128)(2,1)} fusion(bf16[21,16,1024]{2,1,0:T(8,128)(2,1)} %copy.299, s32[16]{0:T(128)S(1)} %fusion.143, bf16[16,16,1024]{2,1,0:T(8,128)(2,1)} %bitcast.234), kind=kCustom, calls=%fused_computation.4 | custom fusion | bytes 1572928 | tf_op jit(solution)/shard_map/scatter | solution.py:138
  134.0 2.9 %scatter_fusion.1 = bf16[21,16,1024]{2,1,0:T(8,128)(2,1)} fusion(bf16[21,16,1024]{2,1,0:T(8,128)(2,1)} %copy-done.5, s32[16]{0:T(128)S(1)} %fusion.143, bf16[16,16,1024]{2,1,0:T(8,128)(2,1)} %bitcast.235), kind=kCustom, calls=%fused_computation.5 | custom fusion | bytes 1572928 | tf_op jit(solution)/shard_map/scatter | solution.py:141
  136.9 2.3 %gather_fusion.1 = bf16[5,16,1024]{2,1,0:T(8,128)(2,1)} fusion(bf16[16,16,1024]{2,1,0:T(8,128)(2,1)} %all-to-all-done.1, s32[1024]{0:T(1024)S(1)} %pad_clamp_fusion), kind=kCustom, calls=%fused_computation.1.clone | custom fusion | bytes 327700 | tf_op jit(solution)/shard_map/jit(_take)/gather | solution.py:97
  139.1 2.3 %gather_fusion.3 = bf16[5,16,1024]{2,1,0:T(8,128)(2,1)} fusion(bf16[16,16,1024]{2,1,0:T(8,128)(2,1)} %all-to-all-done.2, s32[1024]{0:T(1024)S(1)} %pad_clamp_fusion), kind=kCustom, calls=%fused_computation.3.clone | custom fusion | bytes 327700 | tf_op jit(solution)/shard_map/jit(_take)/gather | solution.py:100
  141.4 1.2 broadcast_select_fusion.2
  142.6 1.2 fusion.159
  143.9 1.4 fusion.48
  152.1 1.2 fusion.58
  159.7 1.3 fusion.15
  161.3 1.7 fusion.14
  164.2 2.0 %fusion.13 = bf16[256,4,128]{0,2,1:T(8,128)(2,1)} fusion(f32[256,4,128]{0,2,1:T(8,128)} %fusion.58, f32[256,4]{0,1:T(4,128)S(1)} %add.122, f32[256,4,80]{0,2,1:T(8,128)S(1)} %get-tuple-element.32, f32[256,4]{0,1:T(4,128)S(1)} %max.67, bf16[80,1024]{1,0:T(8,128)(2,1)} %bitcast.258), kind=kOutput, calls=%fused_computation.38 | convolution fusion | flops 21528576 | bytes 1142784 | tf_op jit(solution)/shard_map/tgk,kd->tgd/dot_general | solution.py:123
  167.5 1.7 fusion.12
  169.2 1.1 copy.233
  170.5 1.7 fusion.11
  174.7 1.9 %select_convert_fusion = bf16[256,4096]{1,0:T(8,128)(2,1)} fusion(bf16[256,4096]{1,0:T(8,128)(2,1)S(1)} %constant_dynamic-update-slice_fusion, pred[256]{0:T(512)(128)(4,1)S(1)} %iota_compare_fusion.5), kind=kLoop, calls=%fused_computation.10 | loop fusion | flops 1048576 | bytes 4194560 | tf_op jit(solution)/shard_map/convert_element_type | solution.py:136
  (164 shorter events, 31.0 us)
Async XLA Ops:
  0.6 3.8 %copy-start.28 = (s32[1,5]{1,0:T(1,128)S(1)}, s32[1,5]{1,0:T(1,128)}, u32[]{:S(2)}) copy-start(s32[1,5]{1,0:T(1,128)} %param.22) | copy-start | bytes 64
  0.6 3.8 %copy-start.29 = (s32[1,5]{1,0:T(1,128)S(1)}, s32[1,5]{1,0:T(1,128)}, u32[]{:S(2)}) copy-start(s32[1,5]{1,0:T(1,128)} %param.23) | copy-start | bytes 64
  3.8 63.0 %copy-start.5 = (bf16[21,16,1024]{2,1,0:T(8,128)(2,1)}, bf16[21,16,1024]{2,1,0:T(8,128)(2,1)S(1)}, u32[]{:S(2)}) copy-start(bf16[21,16,1024]{2,1,0:T(8,128)(2,1)S(1)} %copy.300) | copy-start | bytes 2064388
  5.3 23.4 %all-to-all-start = ((bf16[16,1,1]{2,1,0:T(2,128)(2,1)}), bf16[16,1,1]{2,1,0:T(2,128)(2,1)S(1)}, u32[]{:S(2)}, u32[]{:S(2)}) async-start(bf16[16,1,1]{2,1,0:T(2,128)(2,1)} %copy.190), calls=%async_computation | async-start | bytes 16384 | tf_op jit(solution)/shard_map/all_to_all | solution.py:80
  15.2 4.2 %copy-start.16 = (bf16[256,1024]{1,0:T(8,128)(2,1)S(1)}, bf16[256,1024]{1,0:T(8,128)(2,1)}, u32[]{:S(2)}) copy-start(bf16[256,1024]{1,0:T(8,128)(2,1)} %param.16) | copy-start | bytes 1572868
  15.2 4.2 %copy-start.17 = (bf16[256,1024]{1,0:T(8,128)(2,1)S(1)}, bf16[256,1024]{1,0:T(8,128)(2,1)}, u32[]{:S(2)}) copy-start(bf16[256,1024]{1,0:T(8,128)(2,1)} %param.17) | copy-start | bytes 1572868
  15.3 30.1 %copy-start.13 = (bf16[256,512]{0,1:T(8,128)(2,1)}, bf16[256,512]{0,1:T(8,128)(2,1)S(1)}, u32[]{:S(2)}) copy-start(bf16[256,512]{0,1:T(8,128)(2,1)S(1)} %copy.280) | copy-start | bytes 786436
  17.3 29.4 %copy-start.11 = (bf16[256,512]{0,1:T(8,128)(2,1)}, bf16[256,512]{0,1:T(8,128)(2,1)S(1)}, u32[]{:S(2)}) copy-start(bf16[256,512]{0,1:T(8,128)(2,1)S(1)} %copy.278) | copy-start | bytes 786436
  19.0 2.5 %copy-start.27 = (s32[1,16]{1,0:T(1,128)S(1)}, s32[1,16]{1,0:T(1,128)}, u32[]{:S(2)}) copy-start(s32[1,16]{1,0:T(1,128)} %param.24) | copy-start | bytes 196
  19.2 65.5 %copy-start.6 = (bf16[256,512]{0,1:T(8,128)(2,1)}, bf16[256,512]{0,1:T(8,128)(2,1)S(1)}, u32[]{:S(2)}) copy-start(bf16[256,512]{0,1:T(8,128)(2,1)S(1)} %copy.272) | copy-start | bytes 786436
  20.3 6.1 %copy-start.30 = (s32[1,16]{1,0:T(1,128)S(1)}, s32[1,16]{1,0:T(1,128)}, u32[]{:S(2)}) copy-start(s32[1,16]{1,0:T(1,128)} %param.25) | copy-start | bytes 196
  28.7 12.5 %all-to-all-start.3 = ((bf16[16,1,1]{2,1,0:T(2,128)(2,1)}), bf16[16,1,1]{2,1,0:T(2,128)(2,1)S(1)}, u32[]{:S(2)}, u32[]{:S(2)}) async-start(bf16[16,1,1]{2,1,0:T(2,128)(2,1)} %copy.239), calls=%async_computation.3 | async-start | bytes 16384 | tf_op jit(solution)/shard_map/all_to_all | solution.py:85
  41.2 18.5 %all-to-all-start.4 = ((bf16[16,2,8192]{2,1,0:T(2,128)(2,1)}), bf16[16,2,8192]{2,1,0:T(2,128)(2,1)}, u32[]{:S(2)}, u32[]{:S(2)}) async-start(bf16[16,2,8192]{2,1,0:T(2,128)(2,1)} %reshape.400), calls=%async_computation.4 | async-start | bytes 1048576 | tf_op jit(solution)/shard_map/all_to_all | solution.py:83
  59.7 18.5 %all-to-all-start.5 = ((bf16[16,2,8192]{2,1,0:T(2,128)(2,1)}), bf16[16,2,8192]{2,1,0:T(2,128)(2,1)}, u32[]{:S(2)}, u32[]{:S(2)}) async-start(bf16[16,2,8192]{2,1,0:T(2,128)(2,1)} %reshape.402), calls=%async_computation.5 | async-start | bytes 1048576 | tf_op jit(solution)/shard_map/all_to_all | solution.py:84
  68.2 14.3 %copy-start.8 = (bf16[256,512]{0,1:T(8,128)(2,1)S(1)}, bf16[256,512]{0,1:T(8,128)(2,1)}, u32[]{:S(2)}) copy-start(bf16[256,512]{0,1:T(8,128)(2,1)} %copy.274) | copy-start | bytes 786436
  78.2 18.5 %all-to-all-start.1 = ((bf16[16,16,1024]{2,1,0:T(8,128)(2,1)}), bf16[16,16,1024]{2,1,0:T(8,128)(2,1)}, u32[]{:S(2)}, u32[]{:S(2)}) async-start(bf16[16,16,1024]{2,1,0:T(8,128)(2,1)} %get-tuple-element.14), calls=%async_computation.1 | async-start | bytes 1048576 | tf_op jit(solution)/shard_map/all_to_all | solution.py:94
  96.7 42.4 %all-to-all-start.2 = ((bf16[16,16,1024]{2,1,0:T(8,128)(2,1)}), bf16[16,16,1024]{2,1,0:T(8,128)(2,1)}, u32[]{:S(2)}, u32[]{:S(2)}) async-start(bf16[16,16,1024]{2,1,0:T(8,128)(2,1)} %get-tuple-element.13), calls=%async_computation.2 | async-start | bytes 1048576 | tf_op jit(solution)/shard_map/all_to_all | solution.py:95
  141.4 3.9 %copy-start = (f32[256,4,256]{0,2,1:T(8,128)S(1)}, f32[256,4,256]{0,2,1:T(8,128)}, u32[]{:S(2)}) copy-start(f32[256,4,256]{0,2,1:T(8,128)} %get-tuple-element.50) | copy-start | bytes 3145732
  141.4 3.9 %copy-start.18 = (bf16[256,1024]{1,0:T(8,128)(2,1)S(1)}, bf16[256,1024]{1,0:T(8,128)(2,1)}, u32[]{:S(2)}) copy-start(bf16[256,1024]{1,0:T(8,128)(2,1)} %param.17) | copy-start | bytes 1572868
  141.4 4.2 %copy-start.12 = (bf16[256,512]{0,1:T(8,128)(2,1)S(1)}, bf16[256,512]{0,1:T(8,128)(2,1)}, u32[]{:S(2)}) copy-start(bf16[256,512]{0,1:T(8,128)(2,1)} %copy-done.11) | copy-start | bytes 786436
  142.6 15.3 %copy-start.26 = (bf16[5,16,1024]{2,1,0:T(8,128)(2,1)}, bf16[5,16,1024]{2,1,0:T(8,128)(2,1)S(1)}, u32[]{:S(2)}) copy-start(bf16[5,16,1024]{2,1,0:T(8,128)(2,1)S(1)} %get-tuple-element.17) | copy-start | bytes 491524
  145.3 2.6 %copy-start.10 = (bf16[256,512]{0,1:T(8,128)(2,1)S(1)}, bf16[256,512]{0,1:T(8,128)(2,1)}, u32[]{:S(2)}) copy-start(bf16[256,512]{0,1:T(8,128)(2,1)} %copy.276) | copy-start | bytes 786436
  146.7 3.4 %copy-start.9 = (bf16[256,512]{0,1:T(8,128)(2,1)S(1)}, bf16[256,512]{0,1:T(8,128)(2,1)}, u32[]{:S(2)}) copy-start(bf16[256,512]{0,1:T(8,128)(2,1)} %copy.274) | copy-start | bytes 786436
  147.9 2.5 %copy-start.4 = (f32[256,4,256]{0,2,1:T(8,128)S(1)}, f32[256,4,256]{0,2,1:T(8,128)}, u32[]{:S(2)}) copy-start(f32[256,4,256]{0,2,1:T(8,128)} %get-tuple-element.38) | copy-start | bytes 3145732
  149.0 2.7 %copy-start.7 = (bf16[256,512]{0,1:T(8,128)(2,1)S(1)}, bf16[256,512]{0,1:T(8,128)(2,1)}, u32[]{:S(2)}) copy-start(bf16[256,512]{0,1:T(8,128)(2,1)} %copy-done.6) | copy-start | bytes 786436
  150.1 1.8 copy-start.2
  152.1 2.7 %copy-start.15 = (bf16[256,512]{0,1:T(8,128)(2,1)S(1)}, bf16[256,512]{0,1:T(8,128)(2,1)}, u32[]{:S(2)}) copy-start(bf16[256,512]{0,1:T(8,128)(2,1)} %copy.268) | copy-start | bytes 786436
  153.2 1.8 copy-start.3
  153.6 2.7 %copy-start.14 = (bf16[256,512]{0,1:T(8,128)(2,1)S(1)}, bf16[256,512]{0,1:T(8,128)(2,1)}, u32[]{:S(2)}) copy-start(bf16[256,512]{0,1:T(8,128)(2,1)} %copy.266) | copy-start | bytes 786436
  154.8 1.7 copy-start.1
  156.7 1.7 copy-start.20
  156.7 1.8 copy-start.25
  158.2 1.4 copy-start.19
  159.5 1.8 %copy-start.24 = (f32[256,4,128]{0,2,1:T(8,128)S(1)}, f32[256,4,128]{0,2,1:T(8,128)}, u32[]{:S(2)}) copy-start(f32[256,4,128]{0,2,1:T(8,128)} %fusion.56) | copy-start | bytes 1572868
  163.0 4.5 %copy-start.23 = (f32[256,4,128]{0,2,1:T(8,128)S(1)}, f32[256,4,128]{0,2,1:T(8,128)}, u32[]{:S(2)}) copy-start(f32[256,4,128]{0,2,1:T(8,128)} %fusion.60) | copy-start | bytes 1572868
  166.3 4.2 %copy-start.21 = (f32[256,4,128]{0,2,1:T(8,128)S(1)}, f32[256,4,128]{0,2,1:T(8,128)}, u32[]{:S(2)}) copy-start(f32[256,4,128]{0,2,1:T(8,128)} %fusion.62) | copy-start | bytes 1572868
  169.2 4.1 %copy-start.22 = (f32[256,4,128]{0,2,1:T(8,128)S(1)}, f32[256,4,128]{0,2,1:T(8,128)}, u32[]{:S(2)}) copy-start(f32[256,4,128]{0,2,1:T(8,128)} %fusion.64) | copy-start | bytes 1572868
where the time goes:
time: 179 us; the launch traced here: 177 us
  local copies, waits for them, and re-layouts  49 us (27%)
  matrix products  37.2 us (21%)
  waiting for transfers between devices  32.7 us (18%)
  starting transfers between devices  30.5 us (17%)
  other arithmetic  24.3 us (14%)
  between operations  2.89 us (2%)
    unnamed x85, local copies, waits for them, and re-layouts  23.8 us
    dot_general x16, matrix products, score_block(): jnp.einsum('tgd,kd->tgk', query_block, key_slice, preferred_element_type=...  16.9 us
    all_to_all x1, waiting for transfers between devices, shards(): lax.all_to_all(out_keys, 'seq', split_axis=0, concat_axis=0, tiled=True)  11.4 us
    dot_general x8, matrix products, shards(): jnp.einsum('tgk,kd->tgd', prefix_weights.astype(jnp.bfloat16), prefix_val...  10.7 us
    all_to_all x1, waiting for transfers between devices, shards(): lax.all_to_all(send_keys, 'seq', split_axis=0, concat_axis=0, tiled=True)  8.84 us
    dot_general x8, matrix products, shards(): jnp.einsum('tgk,kd->tgd', fresh_weights.astype(jnp.bfloat16), new_values[...  8.28 us
    all_to_all x1, starting transfers between devices, shards(): lax.all_to_all(request.astype(jnp.bfloat16)[:, None], 'seq', split_axis=0...  7.39 us
    all_to_all x1, waiting for transfers between devices, shards(): lax.all_to_all(out_values, 'seq', split_axis=0, concat_axis=0, tiled=True)  7.22 us
  transfers between devices with their start and end apart: 6, of which 4 were waited for; matrix products, arithmetic and copies ran while one was open for 39% of the time, Pallas kernels for 0%

commit v1 on v0

--- a/solution.py
+++ b/solution.py
@@ -1,9 +1,13 @@
+import functools
 import math
 
 import jax
 import jax.numpy as jnp
 from jax import lax
+from jax.experimental import pallas as pl
+from jax.experimental.pallas import tpu as pltpu
 from jax.sharding import PartitionSpec as P
+
 
 HEADS = 32
 KV_HEADS = 8
@@ -32,7 +36,7 @@
     return fresh_parts
 
 
-def shards(
+def general_shards(
     queries,
     new_keys,
     new_values,
@@ -144,6 +148,358 @@
     return (attention_out, pool_keys_out, pool_values_out)
 
 
+SMEM = pl.BlockSpec(memory_space=pltpu.SMEM)
+VMEM = pl.BlockSpec(memory_space=pltpu.VMEM)
+ANY = pl.BlockSpec(memory_space=pl.ANY)
+LOG2E = 1.4426950408889634
+VMEM_GRANT = 20 * 2**20
+
+
+def in_vmem(value):
+    return pltpu.with_memory_space_constraint(value, pltpu.VMEM)
+
+
+def in_hbm(value):
+    return pltpu.with_memory_space_constraint(value, pltpu.HBM)
+
+
+def run_copies(pairs, sems):
+    copies = [pltpu.make_async_copy(src, dst, sems.at[n]) for n, (src, dst) in enumerate(pairs)]
+    for copy in copies:
+        copy.start()
+    for copy in copies:
+        copy.wait()
+
+
+def position():
+    me = lax.axis_index("seq")
+    return me // 2, me % 2
+
+
+def pack_new_kernel(chips, *refs):
+    new_len, tables, (keys, values), outs = refs[0], refs[1:5], refs[5:7], refs[7 : 7 + chips]
+    table, where_page, sems, *small = refs[7 + chips :]
+    run_copies(list(zip(tables, small)), sems)
+    new_holder, new_slot, page_holder, page_slot = small
+    chip, core = position()
+    pages = new_holder.shape[1]
+    rows = keys.shape[0] // pages
+    for i in range(pages):
+        where_page[new_holder[0, i]] = i
+    pairs, places = [], []
+    for r in range(chips):
+        for side in range(2):
+            start = pl.multiple_of(where_page[2 * (chip ^ r) + (core ^ side)] * rows, rows)
+            places.append((r, side, start))
+            pairs.append((keys.at[pl.ds(start, rows), :], outs[r].at[side, 0]))
+            pairs.append((values.at[pl.ds(start, rows), :], outs[r].at[side, 1]))
+    copies = [pltpu.make_async_copy(src, dst, sems.at[n]) for n, (src, dst) in enumerate(pairs)]
+    for copy in copies:
+        copy.start()
+    row = lax.broadcasted_iota(jnp.int32, table.shape, 0)
+    lane = lax.broadcasted_iota(jnp.int32, table.shape, 1)
+    entry = jnp.zeros(table.shape, jnp.int32)
+    for i in range(pages):
+        entry = jnp.where((row == new_holder[0, i]) & (lane == 0), new_slot[0, i], entry)
+    for j in range(page_holder.shape[1]):
+        entry = jnp.where((row == page_holder[0, j]) & (lane == 1), page_slot[0, j] + 1, entry)
+        entry = jnp.where((row == (page_holder[0, j] ^ 1)) & (lane == 2), page_slot[0, j] + 1, entry)
+    table[...] = entry
+    for copy in copies:
+        copy.wait()
+    live = new_len[0]
+    token = lax.broadcasted_iota(jnp.int32, (rows, keys.shape[1]), 0)
+    for r, side, start in places:
+
+        @pl.when(start + rows > live)
+        def _(r=r, side=side, start=start):
+            keep = token + start < live
+            for kv in range(2):
+                outs[r][side, kv] = jnp.where(keep, outs[r][side, kv], 0)
+
+
+def pack_prefix_kernel(chips, table, pool_keys, pool_values, near_keys, near_values, *rest):
+    outs, sems = rest[:chips], rest[chips]
+    chip, core = position()
+    own = (pool_keys, pool_values)
+    near = (near_keys, near_values)
+    slots = [
+        [jnp.maximum(table[2 * (chip ^ r) + core, 1 + side] - 1, 0) for side in range(2)]
+        for r in range(chips)
+    ]
+    copies = [
+        pltpu.make_async_copy(own[kv].at[slots[r][0]], outs[r].at[0, kv], sems.at[2 * r + kv])
+        for r in range(chips)
+        for kv in range(2)
+    ]
+    for copy in copies:
+        copy.start()
+    for r in range(chips):
+        for kv in range(2):
+            outs[r][1, kv] = near[kv][slots[r][1]]
+    for copy in copies:
+        copy.wait()
+
+
+def relay_kernel(chips, *refs):
+    out, sems = refs[chips:]
+    run_copies([(refs[r].at[1], out.at[r]) for r in range(chips)], sems)
+
+
+def scatter_kernel(chips, table, pool_keys, pool_values, *refs):
+    near, far = refs[:chips], refs[chips]
+    keys_out, values_out, taken, sems = refs[chips + 1 :]
+    chip, core = position()
+    slots = pool_keys.shape[0]
+    for s in range(slots):
+        taken[s] = 0
+    pairs = []
+    for r in range(chips):
+        for side in range(2):
+            slot = table[2 * (chip ^ r) + (core ^ side), 0]
+            taken[slot] = 1
+            page = near[r].at[0] if side == 0 else far.at[r]
+            pairs.append((page.at[0], keys_out.at[slot]))
+            pairs.append((page.at[1], values_out.at[slot]))
+    copies = [pltpu.make_async_copy(src, dst, sems.at[n]) for n, (src, dst) in enumerate(pairs)]
+    for copy in copies:
+        copy.start()
+    base = len(copies)
+
+    def kept(s, action):
+        for kv, (pool, dest) in enumerate(((pool_keys, keys_out), (pool_values, values_out))):
+
+            @pl.when(taken[s] == 0)
+            def _():
+                action(pltpu.make_async_copy(pool.at[s], dest.at[s], sems.at[base + 2 * s + kv]))
+
+    for s in range(slots):
+        kept(s, lambda copy: copy.start())
+    for copy in copies:
+        copy.wait()
+    for s in range(slots):
+        kept(s, lambda copy: copy.wait())
+
+
+def heads_of(queries, step, group, first, count):
+    columns = [pl.multiple_of((step * group + h) * HEAD, HEAD) for h in range(group)]
+    return jnp.concatenate(
+        [queries[first : first + count, pl.ds(c, HEAD)] for c in columns], axis=0
+    )
+
+
+def key_scores(keys, queries):
+    return lax.dot_general(
+        keys, queries, (((1,), (1,)), ((), ())), preferred_element_type=jnp.float32
+    )
+
+
+def fresh_kernel(group, queries, keys, values, partial):
+    half = keys.shape[0] // 2
+    step = pl.program_id(0)
+    scale = LOG2E / math.sqrt(HEAD)
+    shape = (half, group * half)
+    key_row = lax.broadcasted_iota(jnp.int32, shape, 0)
+    token = lax.broadcasted_iota(jnp.int32, shape, 1) % half
+    causal = key_row <= token
+    first = pl.multiple_of(step * HEAD, HEAD)
+    head_keys = keys[:, pl.ds(first, HEAD)]
+    values_t = values[:, pl.ds(first, HEAD)].T
+    for part in range(2):
+        count = (part + 1) * half
+        scores = key_scores(head_keys[0:count], heads_of(queries, step, group, part * half, half))
+        pieces = [scores[0:half]] if part else []
+        pieces.append(jnp.where(causal, scores[part * half :], -jnp.inf))
+        top = functools.reduce(jnp.maximum, [jnp.max(p, axis=0, keepdims=True) for p in pieces])
+        weights = [jnp.exp2((p - top) * scale) for p in pieces]
+        total = functools.reduce(jnp.add, [jnp.sum(w, axis=0, keepdims=True) for w in weights])
+        rounded = jnp.concatenate([w.astype(jnp.bfloat16) for w in weights], axis=0)
+        partial[step, part, 0:HEAD] = jnp.dot(
+            values_t[:, 0:count], rounded, preferred_element_type=jnp.float32
+        )
+        partial[step, part, HEAD : HEAD + 1] = top
+        partial[step, part, HEAD + 1 : HEAD + 2] = total
+
+
+def prefix_kernel(chips, group, holder, prefix_len, new_len, queries, partial, *refs):
+    sources, (out, pages, sems) = refs[:chips], refs[chips:]
+    chip, core = position()
+    count, _, rows, _ = pages.shape
+    step = pl.program_id(0)
+
+    @pl.when(step == 0)
+    def _():
+        for j in range(count):
+            source = holder[0, j]
+            rel, side = (source // 2) ^ chip, (source % 2) ^ core
+            for r in range(chips):
+
+                @pl.when(rel == r)
+                def _(r=r, j=j, side=side):
+                    pltpu.make_async_copy(sources[r].at[side], pages.at[j], sems.at[j]).start()
+
+        for j in range(count):
+            pltpu.make_async_copy(sources[0].at[0], pages.at[j], sems.at[j]).wait()
+
+    half = queries.shape[0] // 2
+    tokens = count * rows
+    scale = LOG2E / math.sqrt(HEAD)
+    visible = lax.broadcasted_iota(jnp.int32, (tokens, group * half), 0) < prefix_len[0]
+    lane_token = lax.broadcasted_iota(jnp.int32, (1, group * half), 1) % half
+    first = pl.multiple_of(step * HEAD, HEAD)
+    keys = pages[:, 0, :, pl.ds(first, HEAD)].reshape(tokens, HEAD)
+    values_t = pages[:, 1, :, pl.ds(first, HEAD)].reshape(tokens, HEAD).T
+    for part in range(2):
+        scores = key_scores(keys, heads_of(queries, step, group, part * half, half))
+        scores = jnp.where(visible, scores, -jnp.inf)
+        fresh_top = partial[step, part, HEAD : HEAD + 1]
+        fresh_total = partial[step, part, HEAD + 1 : HEAD + 2]
+        top = jnp.maximum(jnp.max(scores, axis=0, keepdims=True), fresh_top)
+        weights = jnp.exp2((scores - top) * scale)
+        fade = jnp.exp2((fresh_top - top) * scale)
+        total = jnp.sum(weights, axis=0, keepdims=True) + fresh_total * fade
+        share = jnp.where(lane_token + part * half < new_len[0], 1.0 / total, 0.0)
+        weighted = jnp.dot(
+            values_t, weights.astype(jnp.bfloat16), preferred_element_type=jnp.float32
+        )
+        weighted = (weighted + partial[step, part, 0:HEAD] * fade) * share
+        for h in range(group):
+            out[part * half : (part + 1) * half, h * HEAD : (h + 1) * HEAD] = (
+                weighted[:, h * half : (h + 1) * half].T.astype(jnp.bfloat16)
+            )
+
+
+def exchange_shards(
+    queries,
+    new_keys,
+    new_values,
+    pool_keys,
+    pool_values,
+    prefix_len,
+    new_len,
+    page_holder,
+    page_slot,
+    new_holder,
+    new_slot,
+):
+    devices = lax.axis_size("seq")
+    chips = devices // 2
+    local = chips // 2
+    group = HEADS // KV_HEADS
+    span = queries.shape[0]
+    slots, rows, width = pool_keys.shape
+    prefix_pages = page_holder.shape[1]
+    bf16, f32 = jnp.bfloat16, jnp.float32
+    queries = in_vmem(queries)
+    grant = dict(compiler_params=pltpu.CompilerParams(vmem_limit_bytes=VMEM_GRANT))
+    dma = pltpu.SemaphoreType.DMA
+
+    def swap(value, offset):
+        return lax.ppermute(value, "seq", [(i, i ^ offset) for i in range(devices)])
+
+    pair = pltpu.VMEM((2, 2, rows, width), bf16)
+    tables = (new_holder, new_slot, page_holder, page_slot)
+    *packed, table = pl.pallas_call(
+        functools.partial(pack_new_kernel, chips),
+        out_shape=[pair] * chips + [jax.ShapeDtypeStruct((devices, HEAD), jnp.int32)],
+        in_specs=[SMEM] + [ANY] * 6,
+        out_specs=[VMEM] * (chips + 1),
+        scratch_shapes=[pltpu.SMEM((devices,), jnp.int32), dma((4 * chips,))]
+        + [pltpu.SMEM(t.shape, jnp.int32) for t in tables],
+        name="pack_new",
+        **grant,
+    )(new_len, *[in_hbm(t) for t in (*tables, new_keys, new_values)])
+    arrived = [packed[0]] + [None] * (chips - 1)
+    for r in [*range(local, chips), *range(1, local)]:
+        arrived[r] = swap(packed[r], 2 * r)
+    near_keys = swap(pool_keys, 1)
+    near_values = swap(pool_values, 1)
+    table = lax.all_to_all(table, "seq", split_axis=0, concat_axis=0, tiled=True)
+
+    sources = pl.pallas_call(
+        functools.partial(pack_prefix_kernel, chips),
+        out_shape=[pair] * chips,
+        in_specs=[SMEM, ANY, ANY, VMEM, VMEM],
+        out_specs=[VMEM] * chips,
+        scratch_shapes=[dma((2 * chips,))],
+        name="pack_prefix",
+        **grant,
+    )(
+        table,
+        in_hbm(pool_keys),
+        in_hbm(pool_values),
+        in_vmem(near_keys),
+        in_vmem(near_values),
+    )
+    pages = list(sources)
+    for r in [*range(local, chips), *range(1, local)]:
+        pages[r] = swap(sources[r], 2 * r)
+
+    partial = pl.pallas_call(
+        functools.partial(fresh_kernel, group),
+        grid=(KV_HEADS,),
+        out_shape=pltpu.VMEM((KV_HEADS, 2, HEAD + 8, group * span // 2), f32),
+        in_specs=[VMEM] * 3,
+        out_specs=VMEM,
+        cost_estimate=pl.CostEstimate(
+            flops=4 * span * span * HEADS * HEAD,
+            bytes_accessed=8 * span * HEADS * HEAD,
+            transcendentals=span * span * HEADS,
+        ),
+        name="fresh",
+        **grant,
+    )(queries, in_vmem(new_keys), in_vmem(new_values))
+
+    arrived = [in_vmem(a) for a in arrived]
+    relay = pl.pallas_call(
+        functools.partial(relay_kernel, chips),
+        out_shape=pltpu.VMEM((chips, 2, rows, width), bf16),
+        in_specs=[VMEM] * chips,
+        out_specs=VMEM,
+        scratch_shapes=[dma((chips,))],
+        name="relay",
+        **grant,
+    )(*arrived)
+    far = swap(relay, 1)
+    pool_shape = jax.ShapeDtypeStruct(pool_keys.shape, bf16)
+    pool_keys_out, pool_values_out = pl.pallas_call(
+        functools.partial(scatter_kernel, chips),
+        out_shape=[pool_shape] * 2,
+        in_specs=[SMEM] + [VMEM] * (chips + 3),
+        out_specs=[ANY] * 2,
+        scratch_shapes=[pltpu.SMEM((slots,), jnp.int32), dma((4 * chips + 2 * slots,))],
+        name="scatter",
+        **grant,
+    )(table, in_vmem(pool_keys), in_vmem(pool_values), *arrived, in_vmem(far))
+
+    attention_out = pl.pallas_call(
+        functools.partial(prefix_kernel, chips, group),
+        grid=(KV_HEADS,),
+        out_shape=jax.ShapeDtypeStruct((span, HEADS * HEAD), bf16),
+        in_specs=[SMEM] * 3 + [VMEM] * (chips + 2),
+        out_specs=pl.BlockSpec((span, group * HEAD), lambda g: (0, g)),
+        scratch_shapes=[pltpu.VMEM((prefix_pages, 2, rows, width), bf16), dma((prefix_pages,))],
+        name="prefix",
+        **grant,
+    )(
+        page_holder,
+        prefix_len,
+        new_len,
+        queries,
+        in_vmem(partial),
+        *[in_vmem(p) for p in pages],
+    )
+    return (attention_out, pool_keys_out, pool_values_out)
+
+
+def shards(*args):
+    devices = lax.axis_size("seq")
+    new_pages = args[9].shape[1]
+    if devices == new_pages and devices >= 4 and devices & (devices - 1) == 0:
+        return exchange_shards(*args)
+    return general_shards(*args)
+
+
 def solution(mesh):
     in_specs = (
         P(("groups", "seq"), None),
@@ -163,4 +519,6 @@
         P(("groups", "seq"), None, None),
         P(("groups", "seq"), None, None),
     )
-    return jax.shard_map(shards, mesh=mesh, in_specs=in_specs, out_specs=out_specs, check_vma=False)
+    return jax.shard_map(
+        shards, mesh=mesh, in_specs=in_specs, out_specs=out_specs, check_vma=False
+    )

time: 179 us -> 84.1 us (0.47)
  local copies, waits for them, and re-layouts: 49 us -> 0.03 us
  matrix products: 37.2 us -> 0 us
  other arithmetic: 24.3 us -> 0 us
  Pallas kernels: 0 us -> 21.5 us
  waiting for transfers between devices: 32.7 us -> 14.1 us
  blocking collectives: 0 us -> 12.7 us
    dot_general x34 -> x0, matrix products: 37.2 us -> none  [the longest x16 16.9 us: score_block(): jnp.einsum('tgd,kd->tgk', query_block, key_slice, preferred_element_type=...]
    all_to_all x6 -> x0, waiting for transfers between devices: 32.7 us -> none  [the longest x1 11.4 us: shards(): lax.all_to_all(out_keys, 'seq', split_axis=0, concat_axis=0, tiled=True)]
    ppermute x0 -> x17, starting transfers between devices: none -> 32 us  [swap(): return lax.ppermute(value, 'seq', [(i, i ^ offset) for i in range(devices)])]
    all_to_all x6 -> x0, starting transfers between devices: 30.5 us -> none  [the longest x1 7.39 us: shards(): lax.all_to_all(request.astype(jnp.bfloat16)[:, None], 'seq', split_axis=0...]
    unnamed x85 -> x12, local copies, waits for them, and re-layouts: 23.8 us -> 0.03 us
    pallas_call x0 -> x6, Pallas kernels: none -> 21.5 us  [the longest x1 7.84 us: exchange_shards(): pl.pallas_call(functools.partial(prefix_kernel, chips, group), grid=(KV_H...]
    ppermute x0 -> x17, waiting for transfers between devices: none -> 14.1 us  [swap(): return lax.ppermute(value, 'seq', [(i, i ^ offset) for i in range(devices)])]
    all_to_all x4 -> x0, other arithmetic: 13.1 us -> none  [the longest x2 7.06 us: shards(): lax.all_to_all(out_keys, 'seq', split_axis=0, concat_axis=0, tiled=True)]
  transfers between devices with their start and end apart: 6 -> 17, of which waited for: 4 -> 6; matrix products, arithmetic and copies ran while one was open for 39% -> 0% of each run, Pallas kernels for 0% -> 14%
where the time goes in v1:
time: 84.1 us; the launch traced here: 82.4 us
  starting transfers between devices  32 us (38%)
  Pallas kernels  21.5 us (26%)
  waiting for transfers between devices  14.1 us (17%)
  blocking collectives  12.7 us (15%)
  between operations  2.08 us (2%)
    ppermute x17, starting transfers between devices, swap(): return lax.ppermute(value, 'seq', [(i, i ^ offset) for i in range(devices)])  32 us
    ppermute x17, waiting for transfers between devices, swap(): return lax.ppermute(value, 'seq', [(i, i ^ offset) for i in range(devices)])  14.1 us
    all_to_all x1, blocking collectives, exchange_shards(): lax.all_to_all(table, 'seq', split_axis=0, concat_axis=0, tiled=True)  12.7 us
    pallas_call x1, Pallas kernels, exchange_shards(): pl.pallas_call(functools.partial(prefix_kernel, chips, group), grid=(KV_H...  7.84 us
    pallas_call x1, Pallas kernels, exchange_shards(): pl.pallas_call(functools.partial(fresh_kernel, group), grid=(KV_HEADS,),...  6.19 us
    pallas_call x1, Pallas kernels, exchange_shards(): pl.pallas_call(functools.partial(scatter_kernel, chips), out_shape=[pool_...  2.4 us
    pallas_call x1, Pallas kernels, exchange_shards(): pl.pallas_call(functools.partial(pack_new_kernel, chips), out_shape=[pair...  2.31 us
    pallas_call x1, Pallas kernels, exchange_shards(): pl.pallas_call(functools.partial(pack_prefix_kernel, chips), out_shape=[p...  2.02 us
  transfers between devices with their start and end apart: 17, of which 6 were waited for; matrix products, arithmetic and copies ran while one was open for 0% of the time, Pallas kernels for 14%

profile of v1, /device:TPU:0, one launch (start us, length us, event | category | flops | bytes accessed | tf_op | source)
XLA Modules:
  0.0 82.4 jit_solution(6671202089521389209)
XLA Ops:
  1.3 2.3 %pack_new.1 = (bf16[2,2,16,1024]{3,2,1,0:T(8,128)(2,1)S(1)}, bf16[2,2,16,1024]{3,2,1,0:T(8,128)(2,1)S(1)}, bf16[2,2,16,1024]{3,2,1,0:T(8,128)(2,1)S(1)}, bf16[2,...) custom-call(s32[1]{0:T(128)S(6)} %copy.16.refs_0_.new_len, ...), custom_call_target="tpu_custom_call" | custom-call | tf_op jit(solution)/shard_map/pack_new/pallas_call | solution.py:402
  3.6 3.0 %collective-permute-start.9 = (bf16[2,2,16,1024]{3,2,1,0:T(8,128)(2,1)S(1)}, bf16[2,2,16,1024]{3,2,1,0:T(8,128)(2,1)S(1)}, u32[]{:S(2)}, u32[]{:S(2)}) collective-permute-start(bf16[2,2,16,1024]{3,2,1,0:T(8,128)(2,1)S(1)} %get-tuple-element.32), channel_id=1, source_target_pairs={{0,2},{1,3},{2,0},{3,1},{4,6},{5,7},{6,4},{7,5},{8,10},{9,11},{10,... | collective-permute-start | bytes 393224 | tf_op jit(solution)/shard_map/ppermute | solution.py:398
  6.6 0.0 collective-permute-start
  6.6 0.5 collective-permute-start.1
  7.1 1.6 %collective-permute-start.10 = (bf16[2,2,16,1024]{3,2,1,0:T(8,128)(2,1)S(1)}, bf16[2,2,16,1024]{3,2,1,0:T(8,128)(2,1)S(1)}, u32[]{:S(2)}, u32[]{:S(2)}) collective-permute-start(bf16[2,2,16,1024]{3,2,1,0:T(8,128)(2,1)S(1)} %get-tuple-element.33), channel_id=1, source_target_pairs={{0,4},{1,5},{2,6},{3,7},{4,0},{5,1},{6,2},{7,3},{8,12},{9,13},{10,... | collective-permute-start | bytes 393224 | tf_op jit(solution)/shard_map/ppermute | solution.py:398
  8.7 0.0 collective-permute-start.11
  8.7 1.4 %collective-permute-done.9.refs_1_ = bf16[2,2,16,1024]{3,2,1,0:T(8,128)(2,1)S(1)} collective-permute-done((bf16[2,2,16,1024]{3,2,1,0:T(8,128)(2,1)S(1)}, bf16[2,2,16,1024]{3,2,1,0:T(8,128)(2,1)S(1)}, u32[]{:S(2)}, u32[]{:S(2)}) %collective-permute-start.9) | collective-permute-done | bytes 131104 | tf_op jit(solution)/shard_map/ppermute | solution.py:398
  10.1 2.8 %collective-permute-start.12 = (bf16[2,2,16,1024]{3,2,1,0:T(8,128)(2,1)S(1)}, bf16[2,2,16,1024]{3,2,1,0:T(8,128)(2,1)S(1)}, u32[]{:S(2)}, u32[]{:S(2)}) collective-permute-start(bf16[2,2,16,1024]{3,2,1,0:T(8,128)(2,1)S(1)} %get-tuple-element.35), channel_id=1, source_target_pairs={{0,8},{1,9},{2,10},{3,11},{4,12},{5,13},{6,14},{7,15},{8,0},{9,1},... | collective-permute-start | bytes 393224 | tf_op jit(solution)/shard_map/ppermute | solution.py:398
  12.9 3.9 %collective-permute-done.10.refs_2_ = bf16[2,2,16,1024]{3,2,1,0:T(8,128)(2,1)S(1)} collective-permute-done((bf16[2,2,16,1024]{3,2,1,0:T(8,128)(2,1)S(1)}, bf16[2,2,16,1024]{3,2,1,0:T(8,128)(2,1)S(1)}, u32[]{:S(2)}, u32[]{:S(2)}) %collective-permute-start.10) | collective-permute-done | bytes 131104 | tf_op jit(solution)/shard_map/ppermute | solution.py:398
  16.8 0.0 collective-permute-start.13
  16.8 1.3 %collective-permute-done.11.refs_3_ = bf16[2,2,16,1024]{3,2,1,0:T(8,128)(2,1)S(1)} collective-permute-done((bf16[2,2,16,1024]{3,2,1,0:T(8,128)(2,1)S(1)}, bf16[2,2,16,1024]{3,2,1,0:T(8,128)(2,1)S(1)}, u32[]{:S(2)}, u32[]{:S(2)}) %collective-permute-start.11) | collective-permute-done | bytes 131104 | tf_op jit(solution)/shard_map/ppermute | solution.py:398
  18.2 2.2 %collective-permute-start.14 = (bf16[2,2,16,1024]{3,2,1,0:T(8,128)(2,1)S(1)}, bf16[2,2,16,1024]{3,2,1,0:T(8,128)(2,1)S(1)}, u32[]{:S(2)}, u32[]{:S(2)}) collective-permute-start(bf16[2,2,16,1024]{3,2,1,0:T(8,128)(2,1)S(1)} %get-tuple-element.37), channel_id=1, source_target_pairs={{0,12},{1,13},{2,14},{3,15},{4,8},{5,9},{6,10},{7,11},{8,4},{9,5},... | collective-permute-start | bytes 393224 | tf_op jit(solution)/shard_map/ppermute | solution.py:398
  20.3 0.0 collective-permute-done.12.refs_4_
  20.4 10.8 %collective-permute-start.15 = (bf16[2,2,16,1024]{3,2,1,0:T(8,128)(2,1)S(1)}, bf16[2,2,16,1024]{3,2,1,0:T(8,128)(2,1)S(1)}, u32[]{:S(2)}, u32[]{:S(2)}) collective-permute-start(bf16[2,2,16,1024]{3,2,1,0:T(8,128)(2,1)S(1)} %get-tuple-element.38), channel_id=1, source_target_pairs={{0,14},{1,15},{2,12},{3,13},{4,10},{5,11},{6,8},{7,9},{8,6},{9,7},... | collective-permute-start | bytes 393224 | tf_op jit(solution)/shard_map/ppermute | solution.py:398
  31.2 0.0 collective-permute-done.13.refs_5_
  31.2 0.0 collective-permute-done.14.refs_6_
  31.2 3.0 %collective-permute-done.15.refs_7_ = bf16[2,2,16,1024]{3,2,1,0:T(8,128)(2,1)S(1)} collective-permute-done((bf16[2,2,16,1024]{3,2,1,0:T(8,128)(2,1)S(1)}, bf16[2,2,16,1024]{3,2,1,0:T(8,128)(2,1)S(1)}, u32[]{:S(2)}, u32[]{:S(2)}) %collective-permute-start.15) | collective-permute-done | bytes 131104 | tf_op jit(solution)/shard_map/ppermute | solution.py:398
  34.2 0.8 relay.1
  35.0 0.1 collective-permute-start.16
  35.1 12.7 %all_to_all.11 = s32[16,1,128]{2,1,0:T(1,128)S(1)} all-to-all(s32[16,1,128]{2,1,0:T(1,128)S(1)} %bitcast.6), channel_id=1, replica_groups=mesh['groups'=2,'seq'=16] {'seq'}, dimensions={0} | all-to-all | bytes 16384 | tf_op jit(solution)/shard_map/all_to_all | solution.py:417
  47.8 0.0 collective-permute-done.near_keys
  47.8 0.0 collective-permute-done.1.near_values
  47.8 2.0 %pack_prefix.1 = (bf16[2,2,16,1024]{3,2,1,0:T(8,128)(2,1)S(1)}, bf16[2,2,16,1024]{3,2,1,0:T(8,128)(2,1)S(1)}, bf16[2,2,16,1024]{3,2,1,0:T(8,128)(2,1)S(1)}, bf16...) custom-call(s32[16,128]{1,0:T(8,128)S(1)} %bitcast.4, ...), custom_call_target="tpu_custom_call" | custom-call | tf_op jit(solution)/shard_map/pack_prefix/pallas_call | solution.py:419
  49.8 0.5 collective-permute-start.2
  50.4 0.6 collective-permute-start.3
  50.9 2.5 %collective-permute-start.4 = (bf16[2,2,16,1024]{3,2,1,0:T(8,128)(2,1)S(1)}, bf16[2,2,16,1024]{3,2,1,0:T(8,128)(2,1)S(1)}, u32[]{:S(2)}, u32[]{:S(2)}) collective-permute-start(bf16[2,2,16,1024]{3,2,1,0:T(8,128)(2,1)S(1)} %get-tuple-element.26), channel_id=1, source_target_pairs={{0,6},{1,7},{2,4},{3,5},{4,2},{5,3},{6,0},{7,1},{8,14},{9,15},{10,... | collective-permute-start | bytes 393224 | tf_op jit(solution)/shard_map/ppermute | solution.py:398
  53.4 0.5 collective-permute-start.5
  53.9 0.0 collective-permute-done.16.refs_8_
  53.9 2.4 %collective-permute-start.6 = (bf16[2,2,16,1024]{3,2,1,0:T(8,128)(2,1)S(1)}, bf16[2,2,16,1024]{3,2,1,0:T(8,128)(2,1)S(1)}, u32[]{:S(2)}, u32[]{:S(2)}) collective-permute-start(bf16[2,2,16,1024]{3,2,1,0:T(8,128)(2,1)S(1)} %get-tuple-element.28), channel_id=1, source_target_pairs={{0,10},{1,11},{2,8},{3,9},{4,14},{5,15},{6,12},{7,13},{8,2},{9,3},... | collective-permute-start | bytes 393224 | tf_op jit(solution)/shard_map/ppermute | solution.py:398
  56.2 0.0 collective-permute-done.2.refs_1_
  56.2 0.6 collective-permute-start.7
  56.8 1.7 %collective-permute-done.3.refs_2_ = bf16[2,2,16,1024]{3,2,1,0:T(8,128)(2,1)S(1)} collective-permute-done((bf16[2,2,16,1024]{3,2,1,0:T(8,128)(2,1)S(1)}, bf16[2,2,16,1024]{3,2,1,0:T(8,128)(2,1)S(1)}, u32[]{:S(2)}, u32[]{:S(2)}) %collective-permute-start.3) | collective-permute-done | bytes 131104 | tf_op jit(solution)/shard_map/ppermute | solution.py:398
  58.5 4.0 %collective-permute-start.8 = (bf16[2,2,16,1024]{3,2,1,0:T(8,128)(2,1)S(1)}, bf16[2,2,16,1024]{3,2,1,0:T(8,128)(2,1)S(1)}, u32[]{:S(2)}, u32[]{:S(2)}) collective-permute-start(bf16[2,2,16,1024]{3,2,1,0:T(8,128)(2,1)S(1)} %get-tuple-element.30), channel_id=1, source_target_pairs={{0,14},{1,15},{2,12},{3,13},{4,10},{5,11},{6,8},{7,9},{8,6},{9,7},... | collective-permute-start | bytes 393224 | tf_op jit(solution)/shard_map/ppermute | solution.py:398
  63.1 0.0 copy-done
  63.1 0.0 copy-done.3
  63.1 0.0 copy-done.4
  63.2 0.0 copy-start.1
  63.2 0.0 copy-start.2
  63.2 6.2 %fresh.1.partial = f32[8,2,136,512]{3,2,1,0:T(8,128)S(1)} custom-call(bf16[256,4096]{1,0:T(8,128)(2,1)S(1)} %copy-done, bf16[256,1024]{1,0:T(8,128)(2,1)S(1)} %copy-done.3, bf16[256,1024]{1,0:T(8,128)(2,1)S(1)} %copy-done.4), custom_call_target="tpu_custom_call" | custom-call | flops 1073741824 | bytes 8388608 | tf_op jit(solution)/shard_map/fresh/pallas_call | solution.py:438
  69.4 0.0 copy-done.1
  69.4 0.0 copy-start.5
  69.4 2.4 %scatter.1 = (bf16[21,16,1024]{2,1,0:T(8,128)(2,1)}, bf16[21,16,1024]{2,1,0:T(8,128)(2,1)}) custom-call(s32[16,128]{1,0:T(8,128)S(1)} %bitcast.5, bf16[21,16,1024]{2,1,0:T(8,128)(2,1)S(1)} %copy-done.1, bf16[21,16,1024]{2,1,0:T(8,128)(2,1)S(1)} %copy-done.2, bf16[2,2,16,1024]{3,2,1,0:T(8,128)(2,1)S(1)} %get-tuple-element.31.refs_0_, ...), custom_call_target="tpu_custom_call" | custom-call | tf_op jit(solution)/shard_map/scatter/pallas_call | solution.py:465
  71.8 0.0 collective-permute-done.4.refs_3_
  71.8 0.0 collective-permute-done.5.refs_4_
  71.8 2.7 %collective-permute-done.6.refs_5_ = bf16[2,2,16,1024]{3,2,1,0:T(8,128)(2,1)S(1)} collective-permute-done((bf16[2,2,16,1024]{3,2,1,0:T(8,128)(2,1)S(1)}, bf16[2,2,16,1024]{3,2,1,0:T(8,128)(2,1)S(1)}, u32[]{:S(2)}, u32[]{:S(2)}) %collective-permute-start.6) | collective-permute-done | bytes 131104 | tf_op jit(solution)/shard_map/ppermute | solution.py:398
  74.6 0.0 collective-permute-done.7.refs_6_
  74.6 0.0 collective-permute-done.8.refs_7_
  74.6 7.8 %prefix.1 = bf16[256,4096]{1,0:T(8,128)(2,1)} custom-call(s32[1,5]{1,0:T(1,128)S(1)} %copy-done.5, s32[1]{0:T(128)S(6)} %copy.15.prefix_len, s32[1]{0:T(128)S(6)} %copy.16.refs_0_.new_len, bf16[256,4096]{1,0:T(8,128)(2,1)S(1)} %copy-done, f32[8,2,136,512]{3,2,1,0:T(8,128)S(1)} %fresh.1.partial, bf16[2,2,16,1024]{3,2,1,0:T(8,128)(2,1)S(1)} %get-tuple-element.23.refs_0_, ...), custom_call_target="tpu_custom_call" | custom-call | tf_op jit(solution)/shard_map/prefix/pallas_call | solution.py:475
  (5 shorter events, 0.0 us)
Async XLA Ops:
  3.6 6.5 %collective-permute-start.9 = (bf16[2,2,16,1024]{3,2,1,0:T(8,128)(2,1)S(1)}, bf16[2,2,16,1024]{3,2,1,0:T(8,128)(2,1)S(1)}, u32[]{:S(2)}, u32[]{:S(2)}) collective-permute-start(bf16[2,2,16,1024]{3,2,1,0:T(8,128)(2,1)S(1)} %get-tuple-element.32), channel_id=1, source_target_pairs={{0,2},{1,3},{2,0},{3,1},{4,6},{5,7},{6,4},{7,5},{8,10},{9,11},{10,... | collective-permute-start | bytes 393224 | tf_op jit(solution)/shard_map/ppermute | solution.py:398
  6.6 41.2 %collective-permute-start = (bf16[21,16,1024]{2,1,0:T(8,128)(2,1)}, bf16[21,16,1024]{2,1,0:T(8,128)(2,1)S(1)}, u32[]{:S(2)}, u32[]{:S(2)}) collective-permute-start(bf16[21,16,1024]{2,1,0:T(8,128)(2,1)} %pool_keys.3), channel_id=1, source_target_pairs={{0,1},{1,0},{2,3},{3,2},{4,5},{5,4},{6,7},{7,6},{8,9},{9,8},{10,11... | collective-permute-start | bytes 2064392 | tf_op jit(solution)/shard_map/ppermute | solution.py:398
  6.6 41.2 %collective-permute-start.1 = (bf16[21,16,1024]{2,1,0:T(8,128)(2,1)}, bf16[21,16,1024]{2,1,0:T(8,128)(2,1)S(1)}, u32[]{:S(2)}, u32[]{:S(2)}) collective-permute-start(bf16[21,16,1024]{2,1,0:T(8,128)(2,1)} %pool_values.3), channel_id=1, source_target_pairs={{0,1},{1,0},{2,3},{3,2},{4,5},{5,4},{6,7},{7,6},{8,9},{9,8},{10,11... | collective-permute-start | bytes 2064392 | tf_op jit(solution)/shard_map/ppermute | solution.py:398
  7.1 9.7 %collective-permute-start.10 = (bf16[2,2,16,1024]{3,2,1,0:T(8,128)(2,1)S(1)}, bf16[2,2,16,1024]{3,2,1,0:T(8,128)(2,1)S(1)}, u32[]{:S(2)}, u32[]{:S(2)}) collective-permute-start(bf16[2,2,16,1024]{3,2,1,0:T(8,128)(2,1)S(1)} %get-tuple-element.33), channel_id=1, source_target_pairs={{0,4},{1,5},{2,6},{3,7},{4,0},{5,1},{6,2},{7,3},{8,12},{9,13},{10,... | collective-permute-start | bytes 393224 | tf_op jit(solution)/shard_map/ppermute | solution.py:398
  8.7 9.4 %collective-permute-start.11 = (bf16[2,2,16,1024]{3,2,1,0:T(8,128)(2,1)S(1)}, bf16[2,2,16,1024]{3,2,1,0:T(8,128)(2,1)S(1)}, u32[]{:S(2)}, u32[]{:S(2)}) collective-permute-start(bf16[2,2,16,1024]{3,2,1,0:T(8,128)(2,1)S(1)} %get-tuple-element.34), channel_id=1, source_target_pairs={{0,6},{1,7},{2,4},{3,5},{4,2},{5,3},{6,0},{7,1},{8,14},{9,15},{10,... | collective-permute-start | bytes 393224 | tf_op jit(solution)/shard_map/ppermute | solution.py:398
  10.1 10.2 %collective-permute-start.12 = (bf16[2,2,16,1024]{3,2,1,0:T(8,128)(2,1)S(1)}, bf16[2,2,16,1024]{3,2,1,0:T(8,128)(2,1)S(1)}, u32[]{:S(2)}, u32[]{:S(2)}) collective-permute-start(bf16[2,2,16,1024]{3,2,1,0:T(8,128)(2,1)S(1)} %get-tuple-element.35), channel_id=1, source_target_pairs={{0,8},{1,9},{2,10},{3,11},{4,12},{5,13},{6,14},{7,15},{8,0},{9,1},... | collective-permute-start | bytes 393224 | tf_op jit(solution)/shard_map/ppermute | solution.py:398
  16.8 14.4 %collective-permute-start.13 = (bf16[2,2,16,1024]{3,2,1,0:T(8,128)(2,1)S(1)}, bf16[2,2,16,1024]{3,2,1,0:T(8,128)(2,1)S(1)}, u32[]{:S(2)}, u32[]{:S(2)}) collective-permute-start(bf16[2,2,16,1024]{3,2,1,0:T(8,128)(2,1)S(1)} %get-tuple-element.36), channel_id=1, source_target_pairs={{0,10},{1,11},{2,8},{3,9},{4,14},{5,15},{6,12},{7,13},{8,2},{9,3},... | collective-permute-start | bytes 393224 | tf_op jit(solution)/shard_map/ppermute | solution.py:398
  18.2 13.0 %collective-permute-start.14 = (bf16[2,2,16,1024]{3,2,1,0:T(8,128)(2,1)S(1)}, bf16[2,2,16,1024]{3,2,1,0:T(8,128)(2,1)S(1)}, u32[]{:S(2)}, u32[]{:S(2)}) collective-permute-start(bf16[2,2,16,1024]{3,2,1,0:T(8,128)(2,1)S(1)} %get-tuple-element.37), channel_id=1, source_target_pairs={{0,12},{1,13},{2,14},{3,15},{4,8},{5,9},{6,10},{7,11},{8,4},{9,5},... | collective-permute-start | bytes 393224 | tf_op jit(solution)/shard_map/ppermute | solution.py:398
  20.4 13.9 %collective-permute-start.15 = (bf16[2,2,16,1024]{3,2,1,0:T(8,128)(2,1)S(1)}, bf16[2,2,16,1024]{3,2,1,0:T(8,128)(2,1)S(1)}, u32[]{:S(2)}, u32[]{:S(2)}) collective-permute-start(bf16[2,2,16,1024]{3,2,1,0:T(8,128)(2,1)S(1)} %get-tuple-element.38), channel_id=1, source_target_pairs={{0,14},{1,15},{2,12},{3,13},{4,10},{5,11},{6,8},{7,9},{8,6},{9,7},... | collective-permute-start | bytes 393224 | tf_op jit(solution)/shard_map/ppermute | solution.py:398
  34.2 28.9 %copy-start = (bf16[256,4096]{1,0:T(8,128)(2,1)S(1)}, bf16[256,4096]{1,0:T(8,128)(2,1)}, u32[]{:S(2)}) copy-start(bf16[256,4096]{1,0:T(8,128)(2,1)} %queries.3) | copy-start | bytes 6291460
  34.2 28.9 %copy-start.3 = (bf16[256,1024]{1,0:T(8,128)(2,1)S(1)}, bf16[256,1024]{1,0:T(8,128)(2,1)}, u32[]{:S(2)}) copy-start(bf16[256,1024]{1,0:T(8,128)(2,1)} %refs_5_.1) | copy-start | bytes 1572868
  34.2 28.9 %copy-start.4 = (bf16[256,1024]{1,0:T(8,128)(2,1)S(1)}, bf16[256,1024]{1,0:T(8,128)(2,1)}, u32[]{:S(2)}) copy-start(bf16[256,1024]{1,0:T(8,128)(2,1)} %refs_6_.1) | copy-start | bytes 1572868
  35.0 18.8 %collective-permute-start.16 = (bf16[8,2,16,1024]{3,2,1,0:T(8,128)(2,1)S(1)}, bf16[8,2,16,1024]{3,2,1,0:T(8,128)(2,1)S(1)}, u32[]{:S(2)}, u32[]{:S(2)}) collective-permute-start(bf16[8,2,16,1024]{3,2,1,0:T(8,128)(2,1)S(1)} %relay.1), channel_id=1, source_target_pairs={{0,1},{1,0},{2,3},{3,2},{4,5},{5,4},{6,7},{7,6},{8,9},{9,8},{10,11... | collective-permute-start | bytes 1572872 | tf_op jit(solution)/shard_map/ppermute | solution.py:398
  49.8 6.4 %collective-permute-start.2 = (bf16[2,2,16,1024]{3,2,1,0:T(8,128)(2,1)S(1)}, bf16[2,2,16,1024]{3,2,1,0:T(8,128)(2,1)S(1)}, u32[]{:S(2)}, u32[]{:S(2)}) collective-permute-start(bf16[2,2,16,1024]{3,2,1,0:T(8,128)(2,1)S(1)} %get-tuple-element.24), channel_id=1, source_target_pairs={{0,2},{1,3},{2,0},{3,1},{4,6},{5,7},{6,4},{7,5},{8,10},{9,11},{10,... | collective-permute-start | bytes 393224 | tf_op jit(solution)/shard_map/ppermute | solution.py:398
  50.4 8.1 %collective-permute-start.3 = (bf16[2,2,16,1024]{3,2,1,0:T(8,128)(2,1)S(1)}, bf16[2,2,16,1024]{3,2,1,0:T(8,128)(2,1)S(1)}, u32[]{:S(2)}, u32[]{:S(2)}) collective-permute-start(bf16[2,2,16,1024]{3,2,1,0:T(8,128)(2,1)S(1)} %get-tuple-element.25), channel_id=1, source_target_pairs={{0,4},{1,5},{2,6},{3,7},{4,0},{5,1},{6,2},{7,3},{8,12},{9,13},{10,... | collective-permute-start | bytes 393224 | tf_op jit(solution)/shard_map/ppermute | solution.py:398
  50.9 20.9 %collective-permute-start.4 = (bf16[2,2,16,1024]{3,2,1,0:T(8,128)(2,1)S(1)}, bf16[2,2,16,1024]{3,2,1,0:T(8,128)(2,1)S(1)}, u32[]{:S(2)}, u32[]{:S(2)}) collective-permute-start(bf16[2,2,16,1024]{3,2,1,0:T(8,128)(2,1)S(1)} %get-tuple-element.26), channel_id=1, source_target_pairs={{0,6},{1,7},{2,4},{3,5},{4,2},{5,3},{6,0},{7,1},{8,14},{9,15},{10,... | collective-permute-start | bytes 393224 | tf_op jit(solution)/shard_map/ppermute | solution.py:398
  53.4 18.5 %collective-permute-start.5 = (bf16[2,2,16,1024]{3,2,1,0:T(8,128)(2,1)S(1)}, bf16[2,2,16,1024]{3,2,1,0:T(8,128)(2,1)S(1)}, u32[]{:S(2)}, u32[]{:S(2)}) collective-permute-start(bf16[2,2,16,1024]{3,2,1,0:T(8,128)(2,1)S(1)} %get-tuple-element.27), channel_id=1, source_target_pairs={{0,8},{1,9},{2,10},{3,11},{4,12},{5,13},{6,14},{7,15},{8,0},{9,1},... | collective-permute-start | bytes 393224 | tf_op jit(solution)/shard_map/ppermute | solution.py:398
  53.9 20.7 %collective-permute-start.6 = (bf16[2,2,16,1024]{3,2,1,0:T(8,128)(2,1)S(1)}, bf16[2,2,16,1024]{3,2,1,0:T(8,128)(2,1)S(1)}, u32[]{:S(2)}, u32[]{:S(2)}) collective-permute-start(bf16[2,2,16,1024]{3,2,1,0:T(8,128)(2,1)S(1)} %get-tuple-element.28), channel_id=1, source_target_pairs={{0,10},{1,11},{2,8},{3,9},{4,14},{5,15},{6,12},{7,13},{8,2},{9,3},... | collective-permute-start | bytes 393224 | tf_op jit(solution)/shard_map/ppermute | solution.py:398
  56.2 18.4 %collective-permute-start.7 = (bf16[2,2,16,1024]{3,2,1,0:T(8,128)(2,1)S(1)}, bf16[2,2,16,1024]{3,2,1,0:T(8,128)(2,1)S(1)}, u32[]{:S(2)}, u32[]{:S(2)}) collective-permute-start(bf16[2,2,16,1024]{3,2,1,0:T(8,128)(2,1)S(1)} %get-tuple-element.29), channel_id=1, source_target_pairs={{0,12},{1,13},{2,14},{3,15},{4,8},{5,9},{6,10},{7,11},{8,4},{9,5},... | collective-permute-start | bytes 393224 | tf_op jit(solution)/shard_map/ppermute | solution.py:398
  58.5 16.1 %collective-permute-start.8 = (bf16[2,2,16,1024]{3,2,1,0:T(8,128)(2,1)S(1)}, bf16[2,2,16,1024]{3,2,1,0:T(8,128)(2,1)S(1)}, u32[]{:S(2)}, u32[]{:S(2)}) collective-permute-start(bf16[2,2,16,1024]{3,2,1,0:T(8,128)(2,1)S(1)} %get-tuple-element.30), channel_id=1, source_target_pairs={{0,14},{1,15},{2,12},{3,13},{4,10},{5,11},{6,8},{7,9},{8,6},{9,7},... | collective-permute-start | bytes 393224 | tf_op jit(solution)/shard_map/ppermute | solution.py:398
  63.2 6.2 %copy-start.1 = (bf16[21,16,1024]{2,1,0:T(8,128)(2,1)S(1)}, bf16[21,16,1024]{2,1,0:T(8,128)(2,1)}, u32[]{:S(2)}) copy-start(bf16[21,16,1024]{2,1,0:T(8,128)(2,1)} %pool_keys.3) | copy-start | bytes 2064388
  63.2 6.2 %copy-start.2 = (bf16[21,16,1024]{2,1,0:T(8,128)(2,1)S(1)}, bf16[21,16,1024]{2,1,0:T(8,128)(2,1)}, u32[]{:S(2)}) copy-start(bf16[21,16,1024]{2,1,0:T(8,128)(2,1)} %pool_values.3) | copy-start | bytes 2064388
  69.4 5.2 %copy-start.5 = (s32[1,5]{1,0:T(1,128)S(1)}, s32[1,5]{1,0:T(1,128)}, u32[]{:S(2)}) copy-start(s32[1,5]{1,0:T(1,128)} %holder.1) | copy-start | bytes 64

commit v2 on v0

--- a/solution.py
+++ b/solution.py
@@ -1,9 +1,13 @@
+import functools
 import math
 
 import jax
 import jax.numpy as jnp
 from jax import lax
+from jax.experimental import pallas as pl
+from jax.experimental.pallas import tpu as pltpu
 from jax.sharding import PartitionSpec as P
+
 
 HEADS = 32
 KV_HEADS = 8
@@ -32,7 +36,7 @@
     return fresh_parts
 
 
-def shards(
+def general_shards(
     queries,
     new_keys,
     new_values,
@@ -144,6 +148,399 @@
     return (attention_out, pool_keys_out, pool_values_out)
 
 
+SMEM = pl.BlockSpec(memory_space=pltpu.SMEM)
+VMEM = pl.BlockSpec(memory_space=pltpu.VMEM)
+ANY = pl.BlockSpec(memory_space=pl.ANY)
+LOG2E = 1.4426950408889634
+VMEM_GRANT = 12 * 2**20
+
+
+def in_vmem(value):
+    return pltpu.with_memory_space_constraint(value, pltpu.VMEM)
+
+
+def in_hbm(value):
+    return pltpu.with_memory_space_constraint(value, pltpu.HBM)
+
+
+def run_copies(pairs, sems):
+    copies = [pltpu.make_async_copy(src, dst, sems.at[n]) for n, (src, dst) in enumerate(pairs)]
+    for copy in copies:
+        copy.start()
+    for copy in copies:
+        copy.wait()
+
+
+def position():
+    me = lax.axis_index("seq")
+    return me // 2, me % 2
+
+
+def pack_new_kernel(chips, *refs):
+    local = chips // 2
+    new_len, tables, wholes, outs = refs[0], refs[1:5], refs[5:7], refs[7 : 9 + local]
+    table, where_page, sems, *scratch = refs[9 + local :]
+    small, staged = scratch[:4], scratch[4:]
+    sources, dests = [*tables, *wholes], [*small, *staged]
+    copies = [pltpu.make_async_copy(a, b, sems.at[n]) for n, (a, b) in enumerate(zip(sources, dests))]
+    for copy in copies:
+        copy.start()
+    for copy in copies[:4]:
+        copy.wait()
+    new_holder, new_slot, page_holder, page_slot = small
+    chip, core = position()
+    pages = new_holder.shape[1]
+    rows = staged[0].shape[0] // pages
+    for i in range(pages):
+        where_page[new_holder[0, i]] = i
+    row = lax.broadcasted_iota(jnp.int32, table.shape, 0)
+    lane = lax.broadcasted_iota(jnp.int32, table.shape, 1)
+    entry = jnp.zeros(table.shape, jnp.int32)
+    for i in range(pages):
+        entry = jnp.where((row == new_holder[0, i]) & (lane == 0), new_slot[0, i], entry)
+    for j in range(page_holder.shape[1]):
+        entry = jnp.where((row == page_holder[0, j]) & (lane == 1), page_slot[0, j] + 1, entry)
+        entry = jnp.where((row == (page_holder[0, j] ^ 1)) & (lane == 2), page_slot[0, j] + 1, entry)
+    table[...] = entry
+    for copy in copies[4:]:
+        copy.wait()
+    live = new_len[0]
+    token = lax.broadcasted_iota(jnp.int32, (rows, wholes[0].shape[1]), 0)
+    for r in range(chips):
+        for side in range(2):
+            start = pl.multiple_of(where_page[2 * (chip ^ r) + (core ^ side)] * rows, rows)
+            keep = token < live - start
+            if r < local:
+                out = outs[side].at[r]
+            else:
+                out = outs[2 + r - local].at[side]
+            for kv in range(2):
+                page = staged[kv][pl.ds(start, rows), :]
+                out[kv] = jnp.where(keep, page, jnp.zeros_like(page))
+
+
+def pack_prefix_kernel(chips, table, *refs):
+    pools, news, outs = (refs[0:2], refs[2:4]), refs[4:6], refs[6:]
+    local = chips // 2
+    width = pools[0][0].shape[2]
+    chip, core = position()
+    for r in range(chips):
+        for side in range(2):
+            slot = jnp.maximum(table[2 * (chip ^ r) + core, 1 + side] - 1, 0)
+            for kv in range(2):
+                page = pools[side][kv].at[slot]
+                if r < local:
+                    outs[r][side, kv] = page[...]
+                else:
+                    outs[r][side, kv] = page[:, : width // 2]
+                    outs[r + local][side, kv] = page[:, width // 2 :]
+            if 0 < r < local:
+                outs[r][2 + side] = news[side][r]
+
+
+def stage_kernel(*refs):
+    run_copies([(refs[0], refs[2]), (refs[1], refs[3])], refs[4])
+
+
+def relay_kernel(*refs):
+    for r, ref in enumerate(refs[:-1]):
+        refs[-1][r] = ref[1]
+
+
+def page_copies(table, pieces, outs, sems):
+    chip, core = position()
+    copies = []
+    for r, side, page in pieces:
+        slot = table[2 * (chip ^ r) + (core ^ side), 0]
+        for kv in range(2):
+            sem = sems.at[len(copies)]
+            copies.append(pltpu.make_async_copy(page.at[kv], outs[kv].at[slot], sem))
+    return copies
+
+
+def scatter_copies(chips, table, pools, own, met, near, pages, far, outs, taken, kept, sems):
+    local = chips // 2
+    slots = pools[0].shape[0]
+    for s in range(slots):
+        taken[s] = 0
+    for d in range(2 * chips):
+        taken[table[d, 0]] = 1
+    count = jnp.int32(0)
+    for s in range(slots):
+        kept[count] = s
+        count = count + 1 - taken[s]
+    pieces = [(0, 0, own.at[0]), (0, 1, met.at[0])]
+    for r in range(1, local):
+        pieces += [(r, side, pages[r].at[2 + side]) for side in range(2)]
+    for n, ref in enumerate(near):
+        pieces += [(local + n, 0, ref.at[0]), (local + n, 1, far.at[n])]
+    copies = page_copies(table, pieces, outs, sems)
+    for n in range(slots - 2 * chips):
+        for kv in range(2):
+            sem = sems.at[len(copies)]
+            copies.append(pltpu.make_async_copy(pools[kv].at[kept[n]], outs[kv].at[kept[n]], sem))
+    return copies
+
+
+def heads_turned(queries, step, group, first, count):
+    columns = [pl.multiple_of((step * group + h) * HEAD, HEAD) for h in range(group)]
+    return jnp.concatenate(
+        [queries[first : first + count, pl.ds(c, HEAD)].T for c in columns], axis=1
+    )
+
+
+def fresh_kernel(group, queries, keys, values, partial, turned):
+    half = keys.shape[0] // 2
+    step = pl.program_id(0)
+    scale = LOG2E / math.sqrt(HEAD)
+    shape = (half, group * half)
+    key_row = lax.broadcasted_iota(jnp.int32, shape, 0)
+    token = lax.broadcasted_iota(jnp.int32, shape, 1) % half
+    causal = key_row <= token
+    first = pl.multiple_of(step * HEAD, HEAD)
+    head_keys = keys[:, pl.ds(first, HEAD)]
+    values_t = values[:, pl.ds(first, HEAD)].T
+    for part in range(2):
+        count = (part + 1) * half
+        heads = heads_turned(queries, step, group, part * half, half)
+        turned[step, part] = heads
+        scores = jnp.dot(head_keys[0:count], heads, preferred_element_type=jnp.float32)
+        pieces = [scores[0:half]] if part else []
+        pieces.append(jnp.where(causal, scores[part * half :], -jnp.inf))
+        top = functools.reduce(jnp.maximum, [jnp.max(p, axis=0, keepdims=True) for p in pieces])
+        weights = [jnp.exp2((p - top) * scale) for p in pieces]
+        total = functools.reduce(jnp.add, [jnp.sum(w, axis=0, keepdims=True) for w in weights])
+        rounded = jnp.concatenate([w.astype(jnp.bfloat16) for w in weights], axis=0)
+        partial[step, part, 0:HEAD] = jnp.dot(
+            values_t[:, 0:count], rounded, preferred_element_type=jnp.float32
+        )
+        partial[step, part, HEAD : HEAD + 1] = top
+        partial[step, part, HEAD + 1 : HEAD + 2] = total
+
+
+def prefix_kernel(chips, group, late, holder, prefix_len, new_len, turned, partial, *refs):
+    local = chips // 2
+    sources, refs = refs[:chips], refs[chips:]
+    chip, core = position()
+    copies = []
+    if late:
+        _, out, pages, staged, where_page, out_sems = refs
+    else:
+        table, *refs = refs
+        pools, (own, met), near, far = refs[:2], refs[2:4], refs[4 : 4 + local], refs[4 + local]
+        out, *pools_out, pages, staged, where_page, out_sems, taken, kept, sems = refs[5 + local :]
+        copies = scatter_copies(
+            chips, table, pools, own, met, near, sources, far, pools_out, taken, kept, sems
+        )
+        for copy in copies:
+            copy.start()
+    count = holder.shape[0]
+    rows, width = pages.shape[2:]
+    half = turned.shape[3] // group
+    for d in range(2 * chips):
+        where_page[d] = count
+    for j in range(count):
+        where_page[holder[j]] = j
+    for r in range(chips):
+        for side in range(2):
+            page = sources[r].at[side]
+            if r < local:
+                page = page.at[:, :, pl.ds(late * width, width)]
+            pages[where_page[2 * (chip ^ r) + (core ^ side)]] = page[...]
+    tokens = count * rows
+    scale = LOG2E / math.sqrt(HEAD)
+    visible = lax.broadcasted_iota(jnp.int32, (tokens, group * half), 0) < prefix_len[0]
+    lane_token = lax.broadcasted_iota(jnp.int32, (1, group * half), 1) % half
+    heads = width // HEAD
+    for place in range(heads):
+        step = late * heads + place
+        columns = slice(place * HEAD, (place + 1) * HEAD)
+        keys = pages[0:count, 0, :, columns].reshape(tokens, HEAD)
+        values_t = pages[0:count, 1, :, columns].reshape(tokens, HEAD).T
+        for part in range(2):
+            scores = jnp.dot(keys, turned[step, part], preferred_element_type=jnp.float32)
+            scores = jnp.where(visible, scores, -jnp.inf)
+            fresh_top = partial[step, part, HEAD : HEAD + 1]
+            fresh_total = partial[step, part, HEAD + 1 : HEAD + 2]
+            top = jnp.maximum(jnp.max(scores, axis=0, keepdims=True), fresh_top)
+            weights = jnp.exp2((scores - top) * scale)
+            fade = jnp.exp2((fresh_top - top) * scale)
+            total = jnp.sum(weights, axis=0, keepdims=True) + fresh_total * fade
+            share = jnp.where(lane_token + part * half < new_len[0], 1.0 / total, 0.0)
+            weighted = jnp.dot(
+                values_t, weights.astype(jnp.bfloat16), preferred_element_type=jnp.float32
+            )
+            weighted = ((weighted + partial[step, part, 0:HEAD] * fade) * share).astype(jnp.bfloat16)
+            for h in range(group):
+                column = (place * group + h) * HEAD
+                staged[part * half : (part + 1) * half, column : column + HEAD] = weighted[
+                    :, h * half : (h + 1) * half
+                ].T
+        size = group * HEAD
+        source = staged.at[:, pl.ds(place * size, size)]
+        dest = out.at[:, pl.ds(step * size, size)]
+        copy = pltpu.make_async_copy(source, dest, out_sems.at[place])
+        copy.start()
+        copies.append(copy)
+    for copy in copies:
+        copy.wait()
+
+
+def exchange_shards(
+    queries,
+    new_keys,
+    new_values,
+    pool_keys,
+    pool_values,
+    prefix_len,
+    new_len,
+    page_holder,
+    page_slot,
+    new_holder,
+    new_slot,
+):
+    devices = lax.axis_size("seq")
+    chips = devices // 2
+    local = chips // 2
+    group = HEADS // KV_HEADS
+    span = queries.shape[0]
+    slots, rows, width = pool_keys.shape
+    prefix_pages = page_holder.shape[1]
+    bf16, f32 = jnp.bfloat16, jnp.float32
+    queries = in_vmem(queries)
+    grant = dict(compiler_params=pltpu.CompilerParams(vmem_limit_bytes=VMEM_GRANT))
+    dma = pltpu.SemaphoreType.DMA
+
+    def swap(value, offset):
+        return lax.ppermute(value, "seq", [(i, i ^ offset) for i in range(devices)])
+
+    pair = pltpu.VMEM((2, 2, rows, width), bf16)
+    double = pltpu.VMEM((4, 2, rows, width), bf16)
+    part_pair = pltpu.VMEM((2, 2, rows, width // 2), bf16)
+    stack = pltpu.VMEM((local, 2, rows, width), bf16)
+    tables = (new_holder, new_slot, page_holder, page_slot)
+    own, other, *packed, table = pl.pallas_call(
+        functools.partial(pack_new_kernel, chips),
+        out_shape=[stack] * 2
+        + [pair] * local
+        + [jax.ShapeDtypeStruct((devices, HEAD), jnp.int32)],
+        in_specs=[SMEM] + [ANY] * 6,
+        out_specs=[VMEM] * (local + 3),
+        scratch_shapes=[pltpu.SMEM((devices,), jnp.int32), dma((6,))]
+        + [pltpu.SMEM(t.shape, jnp.int32) for t in tables]
+        + [pltpu.VMEM(new_keys.shape, bf16)] * 2,
+        name="pack_new",
+        **grant,
+    )(new_len, *[in_hbm(t) for t in (*tables, new_keys, new_values)])
+    near = [swap(m, 2 * r) for r, m in enumerate(packed, local)]
+    own, met = in_vmem(own), in_vmem(swap(other, 1))
+    near_keys = swap(pool_keys, 1)
+    near_values = swap(pool_values, 1)
+    staged = pl.pallas_call(
+        stage_kernel,
+        out_shape=[pltpu.VMEM(pool_keys.shape, bf16)] * 2,
+        in_specs=[ANY] * 2,
+        out_specs=[VMEM] * 2,
+        scratch_shapes=[dma((2,))],
+        name="stage",
+        **grant,
+    )(in_hbm(pool_keys), in_hbm(pool_values))
+    staged = [in_vmem(p) for p in staged]
+    table = lax.all_to_all(table, "seq", split_axis=0, concat_axis=0, tiled=True)
+
+    sources = pl.pallas_call(
+        functools.partial(pack_prefix_kernel, chips),
+        out_shape=[double if 0 < r < local else pair for r in range(local)]
+        + [part_pair] * (2 * local),
+        in_specs=[SMEM] + [VMEM] * 6,
+        out_specs=[VMEM] * (chips + local),
+        name="pack_prefix",
+        **grant,
+    )(table, *staged, in_vmem(near_keys), in_vmem(near_values), own, met)
+    near_pages = [sources[0]] + [swap(sources[r], 2 * r) for r in range(1, local)]
+    near_pages = [in_vmem(p) for p in near_pages]
+    far_pages = [
+        [in_vmem(swap(sources[r + late * local], 2 * r)) for r in range(local, chips)]
+        for late in range(2)
+    ]
+
+    partial, turned = pl.pallas_call(
+        functools.partial(fresh_kernel, group),
+        grid=(KV_HEADS,),
+        out_shape=[
+            pltpu.VMEM((KV_HEADS, 2, HEAD + 8, group * span // 2), f32),
+            pltpu.VMEM((KV_HEADS, 2, HEAD, group * span // 2), bf16),
+        ],
+        in_specs=[VMEM] * 3,
+        out_specs=[VMEM] * 2,
+        cost_estimate=pl.CostEstimate(
+            flops=4 * span * span * HEADS * HEAD,
+            bytes_accessed=8 * span * HEADS * HEAD,
+            transcendentals=span * span * HEADS,
+        ),
+        name="fresh",
+        **grant,
+    )(queries, in_vmem(new_keys), in_vmem(new_values))
+
+    near = [in_vmem(n) for n in near]
+    relay = pl.pallas_call(
+        relay_kernel,
+        out_shape=pltpu.VMEM((local, 2, rows, width), bf16),
+        in_specs=[VMEM] * local,
+        out_specs=VMEM,
+        name="relay",
+        **grant,
+    )(*near)
+    far = swap(relay, 1)
+    pool_shape = jax.ShapeDtypeStruct(pool_keys.shape, bf16)
+
+    out_shape = jax.ShapeDtypeStruct((span, HEADS * HEAD), bf16)
+    scratch = [
+        pltpu.VMEM((prefix_pages + 1, 2, rows, width // 2), bf16),
+        pltpu.VMEM((span, HEADS * HEAD // 2), bf16),
+        pltpu.SMEM((devices,), jnp.int32),
+        dma((KV_HEADS // 2,)),
+    ]
+    scalars = (page_holder.reshape(prefix_pages), prefix_len, new_len)
+    fresh = (in_vmem(turned), in_vmem(partial))
+    early_out, pool_keys_out, pool_values_out = pl.pallas_call(
+        functools.partial(prefix_kernel, chips, group, 0),
+        out_shape=[out_shape, pool_shape, pool_shape],
+        in_specs=[SMEM] * 3
+        + [VMEM] * (chips + 2)
+        + [SMEM]
+        + [VMEM] * (local + 5),
+        out_specs=[ANY] * 3,
+        scratch_shapes=scratch
+        + [
+            pltpu.SMEM((slots,), jnp.int32),
+            pltpu.SMEM((slots + 1,), jnp.int32),
+            dma((4 * devices + 2 * slots,)),
+        ],
+        name="prefix0",
+        **grant,
+    )(*scalars, *fresh, *near_pages, *far_pages[0], table, *staged, own, met, *near, in_vmem(far))
+    attention_out = pl.pallas_call(
+        functools.partial(prefix_kernel, chips, group, 1),
+        out_shape=out_shape,
+        in_specs=[SMEM] * 3 + [VMEM] * (chips + 2) + [ANY],
+        out_specs=ANY,
+        scratch_shapes=scratch,
+        input_output_aliases={chips + 5: 0},
+        name="prefix1",
+        **grant,
+    )(*scalars, *fresh, *near_pages, *far_pages[1], early_out)
+    return (attention_out, pool_keys_out, pool_values_out)
+
+
+def shards(*args):
+    devices = lax.axis_size("seq")
+    new_pages = args[9].shape[1]
+    if devices == new_pages and devices >= 4 and devices & (devices - 1) == 0:
+        return exchange_shards(*args)
+    return general_shards(*args)
+
+
 def solution(mesh):
     in_specs = (
         P(("groups", "seq"), None),
@@ -163,4 +560,6 @@
         P(("groups", "seq"), None, None),
         P(("groups", "seq"), None, None),
     )
-    return jax.shard_map(shards, mesh=mesh, in_specs=in_specs, out_specs=out_specs, check_vma=False)
+    return jax.shard_map(
+        shards, mesh=mesh, in_specs=in_specs, out_specs=out_specs, check_vma=False
+    )

time: 179 us -> 92.1 us (0.51); the launches traced: 177 us -> 91.8 us
  local copies, waits for them, and re-layouts: 49 us -> 0.69 us
  matrix products: 37.2 us -> 0 us
  other arithmetic: 24.3 us -> 0 us
  Pallas kernels: 0 us -> 20.1 us
  starting transfers between devices: 30.5 us -> 43.3 us
  waiting for transfers between devices: 32.7 us -> 25.6 us
    dot_general x34 -> x0, matrix products: 37.2 us -> none  [the longest x16 16.9 us: score_block(): jnp.einsum('tgd,kd->tgk', query_block, key_slice, preferred_element_type=...]
    ppermute x0 -> x19, starting transfers between devices: none -> 35.3 us  [swap(): return lax.ppermute(value, 'seq', [(i, i ^ offset) for i in range(devices)])]
    all_to_all x6 -> x1, waiting for transfers between devices: 32.7 us -> 5.1 us  [exchange_shards(): lax.all_to_all(table, 'seq', split_axis=0, concat_axis=0, tiled=True)]
    unnamed x85 -> x16, local copies, waits for them, and re-layouts: 23.8 us -> 0.69 us
    all_to_all x6 -> x1, starting transfers between devices: 30.5 us -> 8.02 us  [exchange_shards(): lax.all_to_all(table, 'seq', split_axis=0, concat_axis=0, tiled=True)]
    ppermute x0 -> x19, waiting for transfers between devices: none -> 20.5 us  [swap(): return lax.ppermute(value, 'seq', [(i, i ^ offset) for i in range(devices)])]
    pallas_call x0 -> x7, Pallas kernels: none -> 20.1 us  [the longest x1 6.56 us: exchange_shards(): pl.pallas_call(functools.partial(fresh_kernel, group), grid=(KV_HEADS,),...]
    all_to_all x4 -> x0, other arithmetic: 13.1 us -> none  [the longest x2 7.06 us: shards(): lax.all_to_all(out_keys, 'seq', split_axis=0, concat_axis=0, tiled=True)]
  transfers between devices with their start and end apart: 6 -> 20, of which waited for: 4 -> 6; matrix products, arithmetic and copies ran while one was open for 39% -> 0% of each run, Pallas kernels for 0% -> 18%
where the time goes in v2:
time: 92.1 us; the launch traced here: 91.8 us
  starting transfers between devices  43.3 us (47%)
  waiting for transfers between devices  25.6 us (28%)
  Pallas kernels  20.1 us (22%)
  between operations  2.11 us (2%)
    ppermute x19, starting transfers between devices, swap(): return lax.ppermute(value, 'seq', [(i, i ^ offset) for i in range(devices)])  35.3 us
    ppermute x19, waiting for transfers between devices, swap(): return lax.ppermute(value, 'seq', [(i, i ^ offset) for i in range(devices)])  20.5 us
    all_to_all x1, starting transfers between devices, exchange_shards(): lax.all_to_all(table, 'seq', split_axis=0, concat_axis=0, tiled=True)  8.02 us
    pallas_call x1, Pallas kernels, exchange_shards(): pl.pallas_call(functools.partial(fresh_kernel, group), grid=(KV_HEADS,),...  6.56 us
    pallas_call x1, Pallas kernels, exchange_shards(): pl.pallas_call(functools.partial(prefix_kernel, chips, group, 0), out_sha...  5.18 us
    all_to_all x1, waiting for transfers between devices, exchange_shards(): lax.all_to_all(table, 'seq', split_axis=0, concat_axis=0, tiled=True)  5.1 us
    pallas_call x1, Pallas kernels, exchange_shards(): pl.pallas_call(functools.partial(prefix_kernel, chips, group, 1), out_sha...  3.42 us
    pallas_call x1, Pallas kernels, exchange_shards(): pl.pallas_call(functools.partial(pack_new_kernel, chips), out_shape=[stac...  2.04 us
  transfers between devices with their start and end apart: 20, of which 6 were waited for; matrix products, arithmetic and copies ran while one was open for 0% of the time, Pallas kernels for 18%

profile of v2, /device:TPU:0, one launch (start us, length us, event | category | flops | bytes accessed | tf_op | source)
XLA Modules:
  0.0 91.8 jit_solution(11127599457873351415)
XLA Ops:
  0.6 0.6 collective-permute-start
  1.2 0.1 collective-permute-start.1
  1.9 2.0 %pack_new.1 = (bf16[4,2,16,1024]{3,2,1,0:T(8,128)(2,1)S(1)}, bf16[4,2,16,1024]{3,2,1,0:T(8,128)(2,1)}, bf16[2,2,16,1024]{3,2,1,0:T(8,128)(2,1)S(1)}, bf16[2,2,16...) custom-call(s32[1]{0:T(128)S(6)} %copy.18.refs_0_.new_len, ...), custom_call_target="tpu_custom_call" | custom-call | tf_op jit(solution)/shard_map/pack_new/pallas_call | solution.py:422
  4.0 4.1 %collective-permute-start.14 = (bf16[2,2,16,1024]{3,2,1,0:T(8,128)(2,1)S(1)}, bf16[2,2,16,1024]{3,2,1,0:T(8,128)(2,1)S(1)}, u32[]{:S(2)}, u32[]{:S(2)}) collective-permute-start(bf16[2,2,16,1024]{3,2,1,0:T(8,128)(2,1)S(1)} %get-tuple-element.48), channel_id=1, source_target_pairs={{0,8},{1,9},{2,10},{3,11},{4,12},{5,13},{6,14},{7,15},{8,0},{9,1},... | collective-permute-start | bytes 393224 | tf_op jit(solution)/shard_map/ppermute | solution.py:415
  8.0 1.3 %collective-permute-start.15 = (bf16[2,2,16,1024]{3,2,1,0:T(8,128)(2,1)S(1)}, bf16[2,2,16,1024]{3,2,1,0:T(8,128)(2,1)S(1)}, u32[]{:S(2)}, u32[]{:S(2)}) collective-permute-start(bf16[2,2,16,1024]{3,2,1,0:T(8,128)(2,1)S(1)} %get-tuple-element.49), channel_id=1, source_target_pairs={{0,10},{1,11},{2,8},{3,9},{4,14},{5,15},{6,12},{7,13},{8,2},{9,3},... | collective-permute-start | bytes 393224 | tf_op jit(solution)/shard_map/ppermute | solution.py:415
  9.3 3.6 %collective-permute-start.16 = (bf16[2,2,16,1024]{3,2,1,0:T(8,128)(2,1)S(1)}, bf16[2,2,16,1024]{3,2,1,0:T(8,128)(2,1)S(1)}, u32[]{:S(2)}, u32[]{:S(2)}) collective-permute-start(bf16[2,2,16,1024]{3,2,1,0:T(8,128)(2,1)S(1)} %get-tuple-element.50), channel_id=1, source_target_pairs={{0,12},{1,13},{2,14},{3,15},{4,8},{5,9},{6,10},{7,11},{8,4},{9,5},... | collective-permute-start | bytes 393224 | tf_op jit(solution)/shard_map/ppermute | solution.py:415
  12.9 7.9 %collective-permute-done.14.refs_0_.refs_13_ = bf16[2,2,16,1024]{3,2,1,0:T(8,128)(2,1)S(1)} collective-permute-done((bf16[2,2,16,1024]{3,2,1,0:T(8,128)(2,1)S(1)}, bf16[2,2,16,1024]{3,2,1,0:T(8,128)(2,1)S(1)}, u32[]{:S(2)}, u32[]{:S(2)}) %collective-permute-start.14) | collective-permute-done | bytes 131104 | tf_op jit(solution)/shard_map/ppermute | solution.py:415
  20.8 3.9 %collective-permute-start.17 = (bf16[2,2,16,1024]{3,2,1,0:T(8,128)(2,1)S(1)}, bf16[2,2,16,1024]{3,2,1,0:T(8,128)(2,1)S(1)}, u32[]{:S(2)}, u32[]{:S(2)}) collective-permute-start(bf16[2,2,16,1024]{3,2,1,0:T(8,128)(2,1)S(1)} %get-tuple-element.51), channel_id=1, source_target_pairs={{0,14},{1,15},{2,12},{3,13},{4,10},{5,11},{6,8},{7,9},{8,6},{9,7},... | collective-permute-start | bytes 393224 | tf_op jit(solution)/shard_map/ppermute | solution.py:415
  24.8 0.1 collective-permute-done.15.refs_1_.refs_14_
  24.9 0.0 collective-permute-start.2
  24.9 0.0 collective-permute-done.16.refs_2_.refs_15_
  24.9 3.6 %collective-permute-done.17.refs_3_.refs_16_ = bf16[2,2,16,1024]{3,2,1,0:T(8,128)(2,1)S(1)} collective-permute-done((bf16[2,2,16,1024]{3,2,1,0:T(8,128)(2,1)S(1)}, bf16[2,2,16,1024]{3,2,1,0:T(8,128)(2,1)S(1)}, u32[]{:S(2)}, u32[]{:S(2)}) %collective-permute-start.17) | collective-permute-done | bytes 131104 | tf_op jit(solution)/shard_map/ppermute | solution.py:415
  28.5 0.7 relay.1
  29.2 0.7 copy-done
  29.9 0.0 collective-permute-start.18
  29.9 8.0 %all-to-all-start = ((s32[16,1,128]{2,1,0:T(1,128)}), s32[16,1,128]{2,1,0:T(1,128)S(1)}, u32[]{:S(2)}, u32[]{:S(2)}) async-start(s32[16,1,128]{2,1,0:T(1,128)} %bitcast.2), calls=%async_computation | async-start | bytes 16384 | tf_op jit(solution)/shard_map/all_to_all | solution.py:449
  37.9 1.3 %stage.1 = (bf16[21,16,1024]{2,1,0:T(8,128)(2,1)S(1)}, bf16[21,16,1024]{2,1,0:T(8,128)(2,1)S(1)}) custom-call(bf16[21,16,1024]{2,1,0:T(8,128)(2,1)} %refs_0_.2, bf16[21,16,1024]{2,1,0:T(8,128)(2,1)} %refs_1_.3), custom_call_target="tpu_custom_call" | custom-call | tf_op jit(solution)/shard_map/stage/pallas_call | solution.py:439
  39.3 5.1 %all-to-all-done = s32[16,1,128]{2,1,0:T(1,128)S(1)} async-done(((s32[16,1,128]{2,1,0:T(1,128)}), s32[16,1,128]{2,1,0:T(1,128)S(1)}, u32[]{:S(2)}, u32[]{:S(2)}) %all-to-all-start) | async-done | bytes 8224 | tf_op jit(solution)/shard_map/all_to_all | solution.py:449
  44.4 0.0 collective-permute-done.2.refs_5_.refs_12_
  44.4 0.0 collective-permute-done.refs_2_
  44.4 0.0 collective-permute-done.1.refs_3_
  44.4 0.8 pack_prefix.1
  45.2 0.0 copy-start.1
  45.2 0.0 copy-start.6
  45.2 0.6 collective-permute-start.3
  45.8 0.6 collective-permute-start.4
  46.4 2.4 %collective-permute-start.5 = (bf16[4,2,16,1024]{3,2,1,0:T(8,128)(2,1)S(1)}, bf16[4,2,16,1024]{3,2,1,0:T(8,128)(2,1)S(1)}, u32[]{:S(2)}, u32[]{:S(2)}) collective-permute-start(bf16[4,2,16,1024]{3,2,1,0:T(8,128)(2,1)S(1)} %get-tuple-element.39), channel_id=1, source_target_pairs={{0,6},{1,7},{2,4},{3,5},{4,2},{5,3},{6,0},{7,1},{8,14},{9,15},{10,... | collective-permute-start | bytes 786440 | tf_op jit(solution)/shard_map/ppermute | solution.py:415
  48.8 0.5 collective-permute-start.10
  49.3 0.0 collective-permute-done.18.refs_17_
  49.3 2.3 %collective-permute-start.11 = (bf16[2,2,16,512]{3,2,1,0:T(8,128)(2,1)S(1)}, bf16[2,2,16,512]{3,2,1,0:T(8,128)(2,1)S(1)}, u32[]{:S(2)}, u32[]{:S(2)}) collective-permute-start(bf16[2,2,16,512]{3,2,1,0:T(8,128)(2,1)S(1)} %get-tuple-element.45), channel_id=1, source_target_pairs={{0,10},{1,11},{2,8},{3,9},{4,14},{5,15},{6,12},{7,13},{8,2},{9,3},... | collective-permute-start | bytes 196616 | tf_op jit(solution)/shard_map/ppermute | solution.py:415
  51.6 8.1 %collective-permute-done.10.refs_4_ = bf16[2,2,16,512]{3,2,1,0:T(8,128)(2,1)S(1)} collective-permute-done((bf16[2,2,16,512]{3,2,1,0:T(8,128)(2,1)S(1)}, bf16[2,2,16,512]{3,2,1,0:T(8,128)(2,1)S(1)}, u32[]{:S(2)}, u32[]{:S(2)}) %collective-permute-start.10) | collective-permute-done | bytes 65568 | tf_op jit(solution)/shard_map/ppermute | solution.py:415
  59.8 1.1 %collective-permute-start.12 = (bf16[2,2,16,512]{3,2,1,0:T(8,128)(2,1)S(1)}, bf16[2,2,16,512]{3,2,1,0:T(8,128)(2,1)S(1)}, u32[]{:S(2)}, u32[]{:S(2)}) collective-permute-start(bf16[2,2,16,512]{3,2,1,0:T(8,128)(2,1)S(1)} %get-tuple-element.46), channel_id=1, source_target_pairs={{0,12},{1,13},{2,14},{3,15},{4,8},{5,9},{6,10},{7,11},{8,4},{9,5},... | collective-permute-start | bytes 196616 | tf_op jit(solution)/shard_map/ppermute | solution.py:415
  60.9 0.0 collective-permute-done.11.refs_5_
  60.9 3.6 %collective-permute-start.13 = (bf16[2,2,16,512]{3,2,1,0:T(8,128)(2,1)S(1)}, bf16[2,2,16,512]{3,2,1,0:T(8,128)(2,1)S(1)}, u32[]{:S(2)}, u32[]{:S(2)}) collective-permute-start(bf16[2,2,16,512]{3,2,1,0:T(8,128)(2,1)S(1)} %get-tuple-element.47), channel_id=1, source_target_pairs={{0,14},{1,15},{2,12},{3,13},{4,10},{5,11},{6,8},{7,9},{8,6},{9,7},... | collective-permute-start | bytes 196616 | tf_op jit(solution)/shard_map/ppermute | solution.py:415
  65.2 0.7 collective-permute-done.12.refs_6_
  65.8 2.4 %collective-permute-start.6 = (bf16[2,2,16,512]{3,2,1,0:T(8,128)(2,1)S(1)}, bf16[2,2,16,512]{3,2,1,0:T(8,128)(2,1)S(1)}, u32[]{:S(2)}, u32[]{:S(2)}) collective-permute-start(bf16[2,2,16,512]{3,2,1,0:T(8,128)(2,1)S(1)} %get-tuple-element.40), channel_id=1, source_target_pairs={{0,8},{1,9},{2,10},{3,11},{4,12},{5,13},{6,14},{7,15},{8,0},{9,1},... | collective-permute-start | bytes 196616 | tf_op jit(solution)/shard_map/ppermute | solution.py:415
  68.2 0.0 collective-permute-done.13.refs_7_
  68.2 3.6 %collective-permute-start.7 = (bf16[2,2,16,512]{3,2,1,0:T(8,128)(2,1)S(1)}, bf16[2,2,16,512]{3,2,1,0:T(8,128)(2,1)S(1)}, u32[]{:S(2)}, u32[]{:S(2)}) collective-permute-start(bf16[2,2,16,512]{3,2,1,0:T(8,128)(2,1)S(1)} %get-tuple-element.41), channel_id=1, source_target_pairs={{0,10},{1,11},{2,8},{3,9},{4,14},{5,15},{6,12},{7,13},{8,2},{9,3},... | collective-permute-start | bytes 196616 | tf_op jit(solution)/shard_map/ppermute | solution.py:415
  71.8 0.0 collective-permute-done.3.refs_1_
  71.8 1.6 %collective-permute-start.8 = (bf16[2,2,16,512]{3,2,1,0:T(8,128)(2,1)S(1)}, bf16[2,2,16,512]{3,2,1,0:T(8,128)(2,1)S(1)}, u32[]{:S(2)}, u32[]{:S(2)}) collective-permute-start(bf16[2,2,16,512]{3,2,1,0:T(8,128)(2,1)S(1)} %get-tuple-element.42), channel_id=1, source_target_pairs={{0,12},{1,13},{2,14},{3,15},{4,8},{5,9},{6,10},{7,11},{8,4},{9,5},... | collective-permute-start | bytes 196616 | tf_op jit(solution)/shard_map/ppermute | solution.py:415
  73.4 0.0 collective-permute-done.4.refs_2_
  73.4 3.1 %collective-permute-start.9 = (bf16[2,2,16,512]{3,2,1,0:T(8,128)(2,1)S(1)}, bf16[2,2,16,512]{3,2,1,0:T(8,128)(2,1)S(1)}, u32[]{:S(2)}, u32[]{:S(2)}) collective-permute-start(bf16[2,2,16,512]{3,2,1,0:T(8,128)(2,1)S(1)} %get-tuple-element.43), channel_id=1, source_target_pairs={{0,14},{1,15},{2,12},{3,13},{4,10},{5,11},{6,8},{7,9},{8,6},{9,7},... | collective-permute-start | bytes 196616 | tf_op jit(solution)/shard_map/ppermute | solution.py:415
  76.5 6.6 %fresh.1 = (f32[8,2,136,512]{3,2,1,0:T(8,128)S(1)}, bf16[8,2,128,512]{3,2,1,0:T(8,128)(2,1)S(1)}) custom-call(bf16[256,4096]{1,0:T(8,128)(2,1)S(1)} %copy-done.7, bf16[256,1024]{1,0:T(8,128)(2,1)S(1)} %copy-done.4, bf16[256,1024]{1,0:T(8,128)(2,1)S(1)} %copy-done.5), custom_call_target="tpu_custom_call" | custom-call | flops 1073741824 | bytes 8388608 | tf_op jit(solution)/shard_map/fresh/pallas_call | solution.py:467
  83.1 0.0 collective-permute-done.5.refs_3_
  83.1 5.2 %prefix0.1 = (bf16[256,4096]{1,0:T(8,128)(2,1)}, bf16[21,16,1024]{2,1,0:T(8,128)(2,1)}, bf16[21,16,1024]{2,1,0:T(8,128)(2,1)}) custom-call(s32[5]{0:T(128)S(1)} %bitcast.7, s32[1]{0:T(128)S(6)} %copy.17.prefix_len, s32[1]{0:T(128)S(6)} %copy.18.refs_0_.new_len, bf16[8,2,128,512]{3,2,1,0:T(8,128)(2,1)S(1)} %get-tuple-element.29.turned, ...), custom_call_target="tpu_custom_call" | custom-call | tf_op jit(solution)/shard_map/prefix0/pallas_call | solution.py:506
  88.3 0.0 collective-permute-done.6.refs_4_
  88.3 0.0 collective-permute-done.7.refs_5_
  88.4 3.4 %prefix1.1 = bf16[256,4096]{1,0:T(8,128)(2,1)} custom-call(s32[5]{0:T(128)S(1)} %bitcast.8, s32[1]{0:T(128)S(6)} %copy.17.prefix_len, s32[1]{0:T(128)S(6)} %copy.18.refs_0_.new_len, bf16[8,2,128,512]{3,2,1,0:T(8,128)(2,1)S(1)} %get-tuple-element.29.turned, f32[8,2,136,512]{3,2,1,0:T(8,128)S(1)} %get-tuple-element.30.partial, ...), custom_call_target="tpu_custom_call", output_to_operand_aliasing={{}: (13, {})} | custom-call | tf_op jit(solution)/shard_map/prefix1/pallas_call | solution.py:523
  (15 shorter events, 0.0 us)
Async XLA Ops:
  0.6 43.7 %collective-permute-start = (bf16[21,16,1024]{2,1,0:T(8,128)(2,1)}, bf16[21,16,1024]{2,1,0:T(8,128)(2,1)S(1)}, u32[]{:S(2)}, u32[]{:S(2)}) collective-permute-start(bf16[21,16,1024]{2,1,0:T(8,128)(2,1)} %refs_0_.2), channel_id=1, source_target_pairs={{0,1},{1,0},{2,3},{3,2},{4,5},{5,4},{6,7},{7,6},{8,9},{9,8},{10,11... | collective-permute-start | bytes 2064392 | tf_op jit(solution)/shard_map/ppermute | solution.py:415
  1.2 43.2 %collective-permute-start.1 = (bf16[21,16,1024]{2,1,0:T(8,128)(2,1)}, bf16[21,16,1024]{2,1,0:T(8,128)(2,1)S(1)}, u32[]{:S(2)}, u32[]{:S(2)}) collective-permute-start(bf16[21,16,1024]{2,1,0:T(8,128)(2,1)} %refs_1_.3), channel_id=1, source_target_pairs={{0,1},{1,0},{2,3},{3,2},{4,5},{5,4},{6,7},{7,6},{8,9},{9,8},{10,11... | collective-permute-start | bytes 2064392 | tf_op jit(solution)/shard_map/ppermute | solution.py:415
  4.0 16.8 %collective-permute-start.14 = (bf16[2,2,16,1024]{3,2,1,0:T(8,128)(2,1)S(1)}, bf16[2,2,16,1024]{3,2,1,0:T(8,128)(2,1)S(1)}, u32[]{:S(2)}, u32[]{:S(2)}) collective-permute-start(bf16[2,2,16,1024]{3,2,1,0:T(8,128)(2,1)S(1)} %get-tuple-element.48), channel_id=1, source_target_pairs={{0,8},{1,9},{2,10},{3,11},{4,12},{5,13},{6,14},{7,15},{8,0},{9,1},... | collective-permute-start | bytes 393224 | tf_op jit(solution)/shard_map/ppermute | solution.py:415
  8.0 16.8 %collective-permute-start.15 = (bf16[2,2,16,1024]{3,2,1,0:T(8,128)(2,1)S(1)}, bf16[2,2,16,1024]{3,2,1,0:T(8,128)(2,1)S(1)}, u32[]{:S(2)}, u32[]{:S(2)}) collective-permute-start(bf16[2,2,16,1024]{3,2,1,0:T(8,128)(2,1)S(1)} %get-tuple-element.49), channel_id=1, source_target_pairs={{0,10},{1,11},{2,8},{3,9},{4,14},{5,15},{6,12},{7,13},{8,2},{9,3},... | collective-permute-start | bytes 393224 | tf_op jit(solution)/shard_map/ppermute | solution.py:415
  9.3 15.6 %collective-permute-start.16 = (bf16[2,2,16,1024]{3,2,1,0:T(8,128)(2,1)S(1)}, bf16[2,2,16,1024]{3,2,1,0:T(8,128)(2,1)S(1)}, u32[]{:S(2)}, u32[]{:S(2)}) collective-permute-start(bf16[2,2,16,1024]{3,2,1,0:T(8,128)(2,1)S(1)} %get-tuple-element.50), channel_id=1, source_target_pairs={{0,12},{1,13},{2,14},{3,15},{4,8},{5,9},{6,10},{7,11},{8,4},{9,5},... | collective-permute-start | bytes 393224 | tf_op jit(solution)/shard_map/ppermute | solution.py:415
  20.8 7.7 %collective-permute-start.17 = (bf16[2,2,16,1024]{3,2,1,0:T(8,128)(2,1)S(1)}, bf16[2,2,16,1024]{3,2,1,0:T(8,128)(2,1)S(1)}, u32[]{:S(2)}, u32[]{:S(2)}) collective-permute-start(bf16[2,2,16,1024]{3,2,1,0:T(8,128)(2,1)S(1)} %get-tuple-element.51), channel_id=1, source_target_pairs={{0,14},{1,15},{2,12},{3,13},{4,10},{5,11},{6,8},{7,9},{8,6},{9,7},... | collective-permute-start | bytes 393224 | tf_op jit(solution)/shard_map/ppermute | solution.py:415
  24.9 19.5 %collective-permute-start.2 = (bf16[4,2,16,1024]{3,2,1,0:T(8,128)(2,1)}, bf16[4,2,16,1024]{3,2,1,0:T(8,128)(2,1)S(1)}, u32[]{:S(2)}, u32[]{:S(2)}) collective-permute-start(bf16[4,2,16,1024]{3,2,1,0:T(8,128)(2,1)} %get-tuple-element.35), channel_id=1, source_target_pairs={{0,1},{1,0},{2,3},{3,2},{4,5},{5,4},{6,7},{7,6},{8,9},{9,8},{10,11... | collective-permute-start | bytes 786440 | tf_op jit(solution)/shard_map/ppermute | solution.py:415
  28.5 0.7 copy-start.2
  29.2 0.7 copy-start
  29.9 19.4 %collective-permute-start.18 = (bf16[4,2,16,1024]{3,2,1,0:T(8,128)(2,1)}, bf16[4,2,16,1024]{3,2,1,0:T(8,128)(2,1)}, u32[]{:S(2)}, u32[]{:S(2)}) collective-permute-start(bf16[4,2,16,1024]{3,2,1,0:T(8,128)(2,1)} %relay.1), channel_id=1, source_target_pairs={{0,1},{1,0},{2,3},{3,2},{4,5},{5,4},{6,7},{7,6},{8,9},{9,8},{10,11... | collective-permute-start | bytes 786440 | tf_op jit(solution)/shard_map/ppermute | solution.py:415
  29.9 14.5 %all-to-all-start = ((s32[16,1,128]{2,1,0:T(1,128)}), s32[16,1,128]{2,1,0:T(1,128)S(1)}, u32[]{:S(2)}, u32[]{:S(2)}) async-start(s32[16,1,128]{2,1,0:T(1,128)} %bitcast.2), calls=%async_computation | async-start | bytes 16384 | tf_op jit(solution)/shard_map/all_to_all | solution.py:449
  44.4 32.2 %copy-start.4 = (bf16[256,1024]{1,0:T(8,128)(2,1)S(1)}, bf16[256,1024]{1,0:T(8,128)(2,1)}, u32[]{:S(2)}) copy-start(bf16[256,1024]{1,0:T(8,128)(2,1)} %refs_5_.1) | copy-start | bytes 1572868
  44.4 32.2 %copy-start.5 = (bf16[256,1024]{1,0:T(8,128)(2,1)S(1)}, bf16[256,1024]{1,0:T(8,128)(2,1)}, u32[]{:S(2)}) copy-start(bf16[256,1024]{1,0:T(8,128)(2,1)} %refs_6_.1) | copy-start | bytes 1572868
  44.4 32.2 %copy-start.7 = (bf16[256,4096]{1,0:T(8,128)(2,1)S(1)}, bf16[256,4096]{1,0:T(8,128)(2,1)}, u32[]{:S(2)}) copy-start(bf16[256,4096]{1,0:T(8,128)(2,1)} %queries.1) | copy-start | bytes 6291460
  45.2 37.9 %copy-start.1 = (bf16[2,2,16,1024]{3,2,1,0:T(8,128)(2,1)S(1)}, bf16[2,2,16,1024]{3,2,1,0:T(8,128)(2,1)}, u32[]{:S(2)}) copy-start(bf16[2,2,16,1024]{3,2,1,0:T(8,128)(2,1)} %copy-done) | copy-start | bytes 393220
  45.2 37.9 %copy-start.3 = (bf16[2,2,16,1024]{3,2,1,0:T(8,128)(2,1)S(1)}, bf16[2,2,16,1024]{3,2,1,0:T(8,128)(2,1)}, u32[]{:S(2)}) copy-start(bf16[2,2,16,1024]{3,2,1,0:T(8,128)(2,1)} %copy-done.2) | copy-start | bytes 393220
  45.2 37.9 %copy-start.6 = (s32[1,5]{1,0:T(1,128)S(1)}, s32[1,5]{1,0:T(1,128)}, u32[]{:S(2)}) copy-start(s32[1,5]{1,0:T(1,128)} %refs_3_.1) | copy-start | bytes 64
  45.2 26.6 %collective-permute-start.3 = (bf16[4,2,16,1024]{3,2,1,0:T(8,128)(2,1)S(1)}, bf16[4,2,16,1024]{3,2,1,0:T(8,128)(2,1)S(1)}, u32[]{:S(2)}, u32[]{:S(2)}) collective-permute-start(bf16[4,2,16,1024]{3,2,1,0:T(8,128)(2,1)S(1)} %get-tuple-element.37), channel_id=1, source_target_pairs={{0,2},{1,3},{2,0},{3,1},{4,6},{5,7},{6,4},{7,5},{8,10},{9,11},{10,... | collective-permute-start | bytes 786440 | tf_op jit(solution)/shard_map/ppermute | solution.py:415
  45.8 27.7 %collective-permute-start.4 = (bf16[4,2,16,1024]{3,2,1,0:T(8,128)(2,1)S(1)}, bf16[4,2,16,1024]{3,2,1,0:T(8,128)(2,1)S(1)}, u32[]{:S(2)}, u32[]{:S(2)}) collective-permute-start(bf16[4,2,16,1024]{3,2,1,0:T(8,128)(2,1)S(1)} %get-tuple-element.38), channel_id=1, source_target_pairs={{0,4},{1,5},{2,6},{3,7},{4,0},{5,1},{6,2},{7,3},{8,12},{9,13},{10,... | collective-permute-start | bytes 786440 | tf_op jit(solution)/shard_map/ppermute | solution.py:415
  46.4 36.8 %collective-permute-start.5 = (bf16[4,2,16,1024]{3,2,1,0:T(8,128)(2,1)S(1)}, bf16[4,2,16,1024]{3,2,1,0:T(8,128)(2,1)S(1)}, u32[]{:S(2)}, u32[]{:S(2)}) collective-permute-start(bf16[4,2,16,1024]{3,2,1,0:T(8,128)(2,1)S(1)} %get-tuple-element.39), channel_id=1, source_target_pairs={{0,6},{1,7},{2,4},{3,5},{4,2},{5,3},{6,0},{7,1},{8,14},{9,15},{10,... | collective-permute-start | bytes 786440 | tf_op jit(solution)/shard_map/ppermute | solution.py:415
  48.8 11.0 %collective-permute-start.10 = (bf16[2,2,16,512]{3,2,1,0:T(8,128)(2,1)S(1)}, bf16[2,2,16,512]{3,2,1,0:T(8,128)(2,1)S(1)}, u32[]{:S(2)}, u32[]{:S(2)}) collective-permute-start(bf16[2,2,16,512]{3,2,1,0:T(8,128)(2,1)S(1)} %get-tuple-element.44), channel_id=1, source_target_pairs={{0,8},{1,9},{2,10},{3,11},{4,12},{5,13},{6,14},{7,15},{8,0},{9,1},... | collective-permute-start | bytes 196616 | tf_op jit(solution)/shard_map/ppermute | solution.py:415
  49.3 11.6 %collective-permute-start.11 = (bf16[2,2,16,512]{3,2,1,0:T(8,128)(2,1)S(1)}, bf16[2,2,16,512]{3,2,1,0:T(8,128)(2,1)S(1)}, u32[]{:S(2)}, u32[]{:S(2)}) collective-permute-start(bf16[2,2,16,512]{3,2,1,0:T(8,128)(2,1)S(1)} %get-tuple-element.45), channel_id=1, source_target_pairs={{0,10},{1,11},{2,8},{3,9},{4,14},{5,15},{6,12},{7,13},{8,2},{9,3},... | collective-permute-start | bytes 196616 | tf_op jit(solution)/shard_map/ppermute | solution.py:415
  59.8 6.1 %collective-permute-start.12 = (bf16[2,2,16,512]{3,2,1,0:T(8,128)(2,1)S(1)}, bf16[2,2,16,512]{3,2,1,0:T(8,128)(2,1)S(1)}, u32[]{:S(2)}, u32[]{:S(2)}) collective-permute-start(bf16[2,2,16,512]{3,2,1,0:T(8,128)(2,1)S(1)} %get-tuple-element.46), channel_id=1, source_target_pairs={{0,12},{1,13},{2,14},{3,15},{4,8},{5,9},{6,10},{7,11},{8,4},{9,5},... | collective-permute-start | bytes 196616 | tf_op jit(solution)/shard_map/ppermute | solution.py:415
  60.9 7.4 %collective-permute-start.13 = (bf16[2,2,16,512]{3,2,1,0:T(8,128)(2,1)S(1)}, bf16[2,2,16,512]{3,2,1,0:T(8,128)(2,1)S(1)}, u32[]{:S(2)}, u32[]{:S(2)}) collective-permute-start(bf16[2,2,16,512]{3,2,1,0:T(8,128)(2,1)S(1)} %get-tuple-element.47), channel_id=1, source_target_pairs={{0,14},{1,15},{2,12},{3,13},{4,10},{5,11},{6,8},{7,9},{8,6},{9,7},... | collective-permute-start | bytes 196616 | tf_op jit(solution)/shard_map/ppermute | solution.py:415
  65.8 22.5 %collective-permute-start.6 = (bf16[2,2,16,512]{3,2,1,0:T(8,128)(2,1)S(1)}, bf16[2,2,16,512]{3,2,1,0:T(8,128)(2,1)S(1)}, u32[]{:S(2)}, u32[]{:S(2)}) collective-permute-start(bf16[2,2,16,512]{3,2,1,0:T(8,128)(2,1)S(1)} %get-tuple-element.40), channel_id=1, source_target_pairs={{0,8},{1,9},{2,10},{3,11},{4,12},{5,13},{6,14},{7,15},{8,0},{9,1},... | collective-permute-start | bytes 196616 | tf_op jit(solution)/shard_map/ppermute | solution.py:415
  68.2 20.1 %collective-permute-start.7 = (bf16[2,2,16,512]{3,2,1,0:T(8,128)(2,1)S(1)}, bf16[2,2,16,512]{3,2,1,0:T(8,128)(2,1)S(1)}, u32[]{:S(2)}, u32[]{:S(2)}) collective-permute-start(bf16[2,2,16,512]{3,2,1,0:T(8,128)(2,1)S(1)} %get-tuple-element.41), channel_id=1, source_target_pairs={{0,10},{1,11},{2,8},{3,9},{4,14},{5,15},{6,12},{7,13},{8,2},{9,3},... | collective-permute-start | bytes 196616 | tf_op jit(solution)/shard_map/ppermute | solution.py:415
  71.8 16.5 %collective-permute-start.8 = (bf16[2,2,16,512]{3,2,1,0:T(8,128)(2,1)S(1)}, bf16[2,2,16,512]{3,2,1,0:T(8,128)(2,1)S(1)}, u32[]{:S(2)}, u32[]{:S(2)}) collective-permute-start(bf16[2,2,16,512]{3,2,1,0:T(8,128)(2,1)S(1)} %get-tuple-element.42), channel_id=1, source_target_pairs={{0,12},{1,13},{2,14},{3,15},{4,8},{5,9},{6,10},{7,11},{8,4},{9,5},... | collective-permute-start | bytes 196616 | tf_op jit(solution)/shard_map/ppermute | solution.py:415
  73.4 14.9 %collective-permute-start.9 = (bf16[2,2,16,512]{3,2,1,0:T(8,128)(2,1)S(1)}, bf16[2,2,16,512]{3,2,1,0:T(8,128)(2,1)S(1)}, u32[]{:S(2)}, u32[]{:S(2)}) collective-permute-start(bf16[2,2,16,512]{3,2,1,0:T(8,128)(2,1)S(1)} %get-tuple-element.43), channel_id=1, source_target_pairs={{0,14},{1,15},{2,12},{3,13},{4,10},{5,11},{6,8},{7,9},{8,6},{9,7},... | collective-permute-start | bytes 196616 | tf_op jit(solution)/shard_map/ppermute | solution.py:415
